TPU v7x, 1024 devices: a whole 4x8x16 slice. The times are simulated.
1024 devices in a mesh: seq: 16 (over x, y_hi, core), chan: 64 (over y_lo, z).
Axes of the slice: x: 4, y: 8 (y_hi: 2, y_lo: 4; y = y_hi * 4 + y_lo), z: 16, core: 2. Of those that a mesh axis runs over, the one named last changes fastest.
Arguments:
- features: bfloat16 [3, 4096, 2048], P(None, 'chan', 'seq'), may hold values from -6 to 6
- cotangent: bfloat16 [4096, 2048], P('chan', 'seq'), may hold values from -6 to 6
- long_filter: bfloat16 [4096, 2048], P('chan', 'seq'), may hold values from -0.125 to 0.125
- short_filters: float32 [3, 4096, 3], P(None, 'chan'), may hold values from -3.5 to 3.5
- skip_gain: float32 [4096], P('chan'), may hold values from -4 to 4
Outputs:
- gated_out: bfloat16 [4096, 2048], P('chan', 'seq')
- feature_grad: bfloat16 [3, 4096, 2048], P(None, 'chan', 'seq')
- long_grad: bfloat16 [4096, 2048], P('chan', 'seq')
- short_grad: float32 [3, 4096, 3], P(None, 'chan')
- skip_grad: float32 [4096], P('chan')
All inputs are finite; a program needn't handle non-finite values.
Results may differ from a plain program's by a relative error of at most 0.015.
Values may be sent and summed in bfloat16 or wider, within the bound.
No kernel may reach another device: no remote copies, remote signals or barrier semaphores. Data moves between devices by JAX's collectives and lax.ppermute only.
A program may use at most 32 MiB of HBM per device.

v0:
```python
import math

import jax
import jax.numpy as jnp
from jax import lax
from jax.sharding import Mesh
from jax.sharding import PartitionSpec as P

SEQ = ("seq_0", "seq_1", "seq_2")


inner_length = 128
radix_width = 8


def in_blocks(shard, dim, size):
    dims = shard.shape
    parts = shard.reshape(*dims[:dim], size, dims[dim] // size, *dims[dim + 1 :])
    return jnp.moveaxis(parts, dim, 0)


def in_order(parts, dim):
    dims = list(parts.shape[1:])
    dims[dim] *= parts.shape[0]
    return jnp.moveaxis(parts, 0, dim).reshape(dims)


def exchange_in_order(parts, axes, turns):
    dims = [lax.axis_size(a) for a in axes]
    parts = parts.reshape(*dims, *parts.shape[1:])
    for k in turns:
        parts = lax.all_to_all(parts, axes[k], split_axis=k, concat_axis=k, tiled=True)
    return parts.reshape(-1, *parts.shape[len(axes) :])


def exchange_by_chip(shard, groups, turns, split_dim, concat_dim):
    size = lax.axis_size(groups[0]) * lax.axis_size(groups[1])
    parts = in_blocks(shard, split_dim, size)
    return in_order(exchange_in_order(parts, groups, turns), concat_dim)


def gather_turned(arrays, axis, dims):
    turned = [jnp.moveaxis(a, dim, 0) for a, dim in zip(arrays, dims)]
    both = jnp.concatenate([t.reshape(len(t), -1) for t in turned], axis=1)
    result, at, done = (lax.all_gather(both, axis, axis=0, tiled=True), 0, [])
    for t, dim in zip(turned, dims):
        slab = result[:, at : at + t[0].size].reshape(-1, *t.shape[1:])
        done.append(jnp.moveaxis(slab, 0, dim))
        at += t[0].size
    return tuple(done)


def phase_tables(row_count, col_count, length, direction):
    phase_index = (
        lax.iota(jnp.int32, row_count)[:, None] * lax.iota(jnp.int32, col_count)[None, :] % length
    )
    angles = direction * 2.0 * math.pi / length * phase_index.astype(jnp.float32)
    return (jnp.cos(angles), jnp.sin(angles))


def last_axis(operand, matrix):
    return jnp.einsum("...n,nk->...k", operand, matrix, precision=lax.Precision.HIGH)


def first_axis(operand, matrix):
    return jnp.einsum("...ab,ak->...kb", operand, matrix, precision=lax.Precision.HIGH)


def transform(real_part, imag_part, direction):
    length = real_part.shape[-1]
    if length <= inner_length or length % radix_width != 0:
        cos_table, sin_table = phase_tables(length, length, length, direction)
        return (
            last_axis(real_part, cos_table) - last_axis(imag_part, sin_table),
            last_axis(real_part, sin_table) + last_axis(imag_part, cos_table),
        )
    rest_length = length // radix_width
    grid_shape = real_part.shape[:-1] + (radix_width, rest_length)
    real_grid = real_part.reshape(grid_shape)
    imag_grid = imag_part.reshape(grid_shape)
    cos_table, sin_table = phase_tables(radix_width, radix_width, radix_width, direction)
    section_real = first_axis(real_grid, cos_table) - first_axis(imag_grid, sin_table)
    section_imag = first_axis(real_grid, sin_table) + first_axis(imag_grid, cos_table)
    twist_cos, twist_sin = phase_tables(radix_width, rest_length, length, direction)
    turned_real = section_real * twist_cos - section_imag * twist_sin
    turned_imag = section_real * twist_sin + section_imag * twist_cos
    inner_real, inner_imag = transform(turned_real, turned_imag, direction)
    return (
        jnp.swapaxes(inner_real, -1, -2).reshape(real_part.shape),
        jnp.swapaxes(inner_imag, -1, -2).reshape(real_part.shape),
    )


def spectral(mixed_term, gated_grad, kernel, local_gain):
    length = mixed_term.shape[-1]
    mixed_wide = mixed_term.astype(jnp.float32)
    gated_wide = gated_grad.astype(jnp.float32)
    kernel_wide = kernel.astype(jnp.float32)
    extend = ((0, 0), (0, length))
    real_in = jnp.stack([jnp.pad(mixed_wide, extend), jnp.pad(kernel_wide, extend)])
    imag_in = jnp.stack(
        [jnp.pad(gated_wide, extend), jnp.zeros((kernel_wide.shape[0], 2 * length), jnp.float32)]
    )
    freq_real, freq_imag = transform(real_in, imag_in, -1.0)
    packed_real = freq_real[0]
    packed_imag = freq_imag[0]
    mirror_real = jnp.roll(jnp.flip(packed_real, -1), 1, -1)
    mirror_imag = jnp.roll(jnp.flip(packed_imag, -1), 1, -1)
    mix_real = 0.5 * (packed_real + mirror_real)
    mix_imag = 0.5 * (packed_imag - mirror_imag)
    grad_real = 0.5 * (packed_imag + mirror_imag)
    grad_imag = 0.5 * (mirror_real - packed_real)
    kern_real = freq_real[1]
    kern_imag = freq_imag[1]
    conv_real = mix_real * kern_real - mix_imag * kern_imag
    conv_imag = mix_real * kern_imag + mix_imag * kern_real
    corr_real = grad_real * kern_real + grad_imag * kern_imag
    corr_imag = grad_imag * kern_real - grad_real * kern_imag
    cross_real = grad_real * mix_real + grad_imag * mix_imag
    cross_imag = grad_imag * mix_real - grad_real * mix_imag
    back_real = jnp.stack([conv_real - corr_imag, cross_real])
    back_imag = jnp.stack([conv_imag + corr_real, cross_imag])
    time_real, time_imag = transform(back_real, back_imag, 1.0)
    inverse_scale = 1.0 / (2 * length)
    conv_part = time_real[0, :, :length] * inverse_scale
    corr_part = time_imag[0, :, :length] * inverse_scale
    cross_part = time_real[1, :, :length] * inverse_scale
    gain_column = local_gain[:, None]
    long_out = (conv_part + gain_column * mixed_wide).astype(jnp.bfloat16)
    mixed_grad = (corr_part + gain_column * gated_wide).astype(jnp.bfloat16)
    return (long_out, mixed_grad, cross_part.astype(jnp.bfloat16))


def featurize(history, weights, margin, span_count):
    running = weights[:, :, 0:1] * history[:, :, margin : margin + span_count]
    for offset in range(1, margin + 1):
        running = (
            running
            + weights[:, :, offset : offset + 1]
            * history[:, :, margin - offset : margin - offset + span_count]
        )
    return running


def unfeaturize(padded_grad, weights, span_count):
    running = weights[:, :, 0:1] * padded_grad[:, :, 0:span_count]
    for offset in range(1, weights.shape[2]):
        running = (
            running
            + weights[:, :, offset : offset + 1] * padded_grad[:, :, offset : offset + span_count]
        )
    return running


def tap_grads(primed_grad, history, margin, span_count):
    columns = []
    for offset in range(margin + 1):
        columns.append(
            jnp.sum(
                primed_grad * history[:, :, margin - offset : margin - offset + span_count], axis=-1
            )
        )
    return jnp.stack(columns, axis=-1)


def shards(features, cotangent, long_filter, short_filters, skip_gain):
    groups = lax.axis_size(SEQ)
    seq_index = lax.axis_index(SEQ)
    channels = features.shape[1]
    per_group = channels // groups
    margin = short_filters.shape[2] - 1
    local_gain = lax.dynamic_slice_in_dim(skip_gain, seq_index * per_group, per_group, 0)
    stacked = jnp.concatenate([features, cotangent[None], long_filter[None]], 0)
    columns = lax.all_to_all(stacked, SEQ, split_axis=1, concat_axis=2, tiled=True)
    weights = lax.dynamic_slice_in_dim(short_filters, seq_index * per_group, per_group, 1)
    length = columns.shape[2]
    history = jnp.pad(columns[:3].astype(jnp.float32), ((0, 0), (0, 0), (margin, 0)))
    primed = featurize(history, weights, margin, length)
    mixed_term = (primed[1] * primed[2]).astype(jnp.bfloat16)
    cot_wide = columns[3].astype(jnp.float32)
    gated_grad = (cot_wide * primed[0]).astype(jnp.bfloat16)
    long_out, mixed_grad, kernel_grad = spectral(mixed_term, gated_grad, columns[4], local_gain)
    long_wide = long_out.astype(jnp.float32)
    mixed_back = mixed_grad.astype(jnp.float32)
    gated_out = (primed[0] * long_wide).astype(jnp.bfloat16)
    primed_grad = jnp.stack([cot_wide * long_wide, mixed_back * primed[2], mixed_back * primed[1]])
    padded_grad = jnp.pad(primed_grad, ((0, 0), (0, 0), (0, margin)))
    feature_grad = unfeaturize(padded_grad, weights, length).astype(jnp.bfloat16)
    taps_grad = tap_grads(primed_grad, history, margin, length)
    gain_grad = jnp.sum(gated_grad.astype(jnp.float32) * mixed_term.astype(jnp.float32), axis=-1)
    results = jnp.concatenate([gated_out[None], feature_grad, kernel_grad[None]], 0)
    row_blocks = exchange_by_chip(results, (("seq_0", "seq_1"), "seq_2"), (1, 0), 2, 1)
    short_grad, skip_grad = gather_turned((taps_grad, gain_grad), SEQ, (1, 0))
    return (row_blocks[0], row_blocks[1:4], row_blocks[4], short_grad, skip_grad)


def solution(mesh):
    torus = Mesh(
        mesh.devices.reshape(4, 2, 2, mesh.shape["chan"]), ("seq_0", "seq_1", "seq_2", "chan")
    )
    return jax.shard_map(
        shards,
        mesh=torus,
        in_specs=(
            P(None, "chan", SEQ),
            P("chan", SEQ),
            P("chan", SEQ),
            P(None, "chan", None),
            P("chan"),
        ),
        out_specs=(
            P("chan", SEQ),
            P(None, "chan", SEQ),
            P("chan", SEQ),
            P(None, "chan", None),
            P("chan"),
        ),
        check_vma=False,
    )
```

profile of v0, /device:TPU:1, one launch (start us, length us, event | category | flops | bytes accessed | tf_op | source)
XLA Modules:
  0.0 109.6 jit_solution(13664220281029838333)
XLA Ops:
  0.6 0.7 copy.127
  1.4 0.7 copy.128
  2.1 0.8 copy.126
  3.0 0.8 pad_maximum_fusion
  3.7 17.4 %all-to-all-start = ((bf16[5,64,128]{2,0,1:T(8,128)(2,1)}), bf16[5,64,128]{2,0,1:T(8,128)(2,1)S(1)}, u32[]{:S(2)}, u32[]{:S(2)}) async-start(bf16[5,64,128]{2,0,1:T(8,128)(2,1)} %pad_maximum_fusion), calls=%async_computation | async-start | bytes 262144 | tf_op jit(solution)/shard_map/all_to_all | solution.py:174
  21.3 0.9 constant_dynamic-slice_fusion.1
  22.2 0.7 multiply_sine_fusion.8
  22.9 1.3 %dynamic_slice.7 = f32[4]{0:T(128)} dynamic-slice(f32[64]{0:T(128)} %param.9, s32[]{:T(128)S(6)} %select_n.139), dynamic_slice_sizes={4} | dynamic-slice | bytes 36 | tf_op jit(solution)/shard_map/dynamic_slice | solution.py:172
  24.2 0.7 multiply_sine_fusion.6
  24.9 6.4 %all-to-all-done = bf16[5,64,128]{2,0,1:T(8,128)(2,1)S(1)} async-done(((bf16[5,64,128]{2,0,1:T(8,128)(2,1)}), bf16[5,64,128]{2,0,1:T(8,128)(2,1)S(1)}, u32[]{:S(2)}, u32[]{:S(2)}) %all-to-all-start) | async-done | bytes 81952 | tf_op jit(solution)/shard_map/all_to_all | solution.py:174
  32.2 0.7 multiply_reduce_fusion.2
  38.0 1.2 %reshape.560 = f32[2,4,8,512]{3,2,1,0:T(8,128)S(1)} reshape(f32[2,4,8,64,8]{4,3,2,1,0:T(8,128)S(1)} %copy.130) | data formatting | bytes 262144 | tf_op jit(solution)/shard_map/reshape | solution.py:89
  40.1 1.1 %squeeze.36 = f32[1,4,8,512]{3,2,1,0:T(8,128)} reshape(f32[1,4,512,8]{3,2,1,0:T(8,128)S(1)} %copy.131) | data formatting | bytes 131072 | tf_op jit(solution)/shard_map/squeeze | solution.py:105
  43.0 1.2 %reshape.561 = f32[2,4,8,512]{3,2,1,0:T(8,128)S(1)} reshape(f32[2,4,8,64,8]{4,3,2,1,0:T(8,128)S(1)} %copy.135) | data formatting | bytes 262144 | tf_op jit(solution)/shard_map/reshape | solution.py:90
  45.7 2.8 %reverse.4 = f32[4,4096]{1,0:T(4,128)S(1)} reverse(f32[4,4096]{1,0:T(4,128)S(1)} %bitcast.330), dimensions={1} | reverse | bytes 131072
  49.5 2.8 %reverse.5 = f32[4,4096]{1,0:T(4,128)S(1)} reverse(f32[4,4096]{1,0:T(4,128)S(1)} %bitcast.331), dimensions={1} | reverse | bytes 131072
  58.4 1.2 %reshape.564 = f32[2,4,8,512]{3,2,1,0:T(8,128)S(1)} reshape(f32[2,4,8,64,8]{4,3,2,1,0:T(8,128)S(1)} %copy.140) | data formatting | bytes 262144 | tf_op jit(solution)/shard_map/reshape | solution.py:89
  60.2 1.2 %reshape.566 = f32[2,4,8,512]{3,2,1,0:T(8,128)S(1)} reshape(f32[2,4,8,64,8]{4,3,2,1,0:T(8,128)S(1)} %copy.142) | data formatting | bytes 262144 | tf_op jit(solution)/shard_map/reshape | solution.py:90
  62.0 1.1 %reshape.567 = f32[2,4,4096]{2,1,0:T(4,128)S(1)} reshape(f32[2,4,512,8]{3,2,1,0:T(8,128)S(1)} %copy.143) | data formatting | bytes 262144 | tf_op jit(solution)/shard_map/reshape | solution.py:90
  63.8 1.1 %reshape.565 = f32[2,4,4096]{2,1,0:T(4,128)S(1)} reshape(f32[2,4,512,8]{3,2,1,0:T(8,128)S(1)} %copy.141) | data formatting | bytes 262144 | tf_op jit(solution)/shard_map/reshape | solution.py:89
  65.7 4.1 %all_to_all.25 = bf16[8,2,5,4,128]{4,0,3,2,1:T(8,128)(2,1)S(1)} all-to-all(bf16[8,2,5,4,128]{4,0,3,2,1:T(8,128)(2,1)S(1)} %copy.144), channel_id=1, replica_groups=mesh['seq_0'=4,'seq_1'=2,'seq_2'=2,'chan'=64] {'seq_2'}, dimensions={1} | all-to-all | bytes 163840 | tf_op jit(solution)/shard_map/all_to_all | solution.py:32
  69.8 0.7 copy.145
  70.5 3.4 %all-to-all-start.2 = ((bf16[8,2,5,4,128]{4,1,3,2,0:T(2,128)(2,1)}), bf16[8,2,5,4,128]{4,1,3,2,0:T(2,128)(2,1)S(1)}, u32[]{:S(2)}, u32[]{:S(2)}) async-start(bf16[8,2,5,4,128]{4,1,3,2,0:T(2,128)(2,1)} %copy.145), calls=%async_computation.2 | async-start | bytes 163840 | tf_op jit(solution)/shard_map/all_to_all | solution.py:32
  74.3 32.0 %all-gather = f32[16,4,10]{2,1,0:T(4,128)S(1)} all-gather(f32[1,4,10]{2,1,0:T(4,128)S(1)} %maximum_bitcast_fusion.1), channel_id=1, replica_groups=mesh['seq_0'=4,'seq_1'=2,'seq_2'=2,'chan'=64] {'seq_0','seq_1','seq_2'}, dimensions={0}, use_global_device_ids=true | all-gather | bytes 2720 | tf_op jit(solution)/shard_map/all_gather | solution.py:45
  (146 shorter events, 23.1 us)
Async XLA Ops:
  3.7 27.5 %all-to-all-start = ((bf16[5,64,128]{2,0,1:T(8,128)(2,1)}), bf16[5,64,128]{2,0,1:T(8,128)(2,1)S(1)}, u32[]{:S(2)}, u32[]{:S(2)}) async-start(bf16[5,64,128]{2,0,1:T(8,128)(2,1)} %pad_maximum_fusion), calls=%async_computation | async-start | bytes 262144 | tf_op jit(solution)/shard_map/all_to_all | solution.py:174
  21.2 15.8 %copy-start.6 = (f32[8,64]{1,0:T(8,128)}, f32[8,64]{1,0:T(8,128)S(1)}, u32[]{:S(2)}) copy-start(f32[8,64]{1,0:T(8,128)S(1)} %get-tuple-element.46) | copy-start | bytes 6148
  21.2 15.8 %copy-start.8 = (f32[8,64]{1,0:T(8,128)}, f32[8,64]{1,0:T(8,128)S(1)}, u32[]{:S(2)}) copy-start(f32[8,64]{1,0:T(8,128)S(1)} %get-tuple-element.47) | copy-start | bytes 6148
  22.2 12.5 %copy-start.12 = (f32[3,4]{1,0:T(4,128)}, f32[3,4]{1,0:T(4,128)S(1)}, u32[]{:S(2)}) copy-start(f32[3,4]{1,0:T(4,128)S(1)} %get-tuple-element.42) | copy-start | bytes 148
  22.2 12.5 %copy-start.14 = (f32[3,4]{1,0:T(4,128)}, f32[3,4]{1,0:T(4,128)S(1)}, u32[]{:S(2)}) copy-start(f32[3,4]{1,0:T(4,128)S(1)} %get-tuple-element.43) | copy-start | bytes 148
  24.2 10.5 %copy-start.16 = (f32[3,4,1]{1,0,2:T(4,128)}, f32[3,4,1]{1,0,2:T(4,128)S(1)}, u32[]{:S(2)}) copy-start(f32[3,4,1]{1,0,2:T(4,128)S(1)} %copy.212) | copy-start | bytes 148
  32.9 0.6 copy-start.1
  39.2 2.7 %copy-start.7 = (f32[8,64]{1,0:T(8,128)S(1)}, f32[8,64]{1,0:T(8,128)}, u32[]{:S(2)}) copy-start(f32[8,64]{1,0:T(8,128)} %copy-done.6) | copy-start | bytes 6148
  39.2 2.7 %copy-start.9 = (f32[8,64]{1,0:T(8,128)S(1)}, f32[8,64]{1,0:T(8,128)}, u32[]{:S(2)}) copy-start(f32[8,64]{1,0:T(8,128)} %copy-done.8) | copy-start | bytes 6148
  48.6 4.7 %copy-start.18 = (f32[1,4,1]{2,1,0:T(4,128)S(1)}, f32[1,4,1]{2,1,0:T(4,128)}, u32[]{:S(2)}) copy-start(f32[1,4,1]{2,1,0:T(4,128)} %slice_bitcast_fusion.2) | copy-start | bytes 52
  48.9 4.6 %copy-start = (f32[1,4,8,512]{3,2,1,0:T(8,128)S(1)}, f32[1,4,8,512]{3,2,1,0:T(8,128)}, u32[]{:S(2)}) copy-start(f32[1,4,8,512]{3,2,1,0:T(8,128)} %squeeze.36) | copy-start | bytes 196612
  52.4 2.0 %copy-start.10 = (f32[8,512]{1,0:T(8,128)S(1)}, f32[8,512]{1,0:T(8,128)}, u32[]{:S(2)}) copy-start(f32[8,512]{1,0:T(8,128)} %get-tuple-element.48) | copy-start | bytes 49156
  52.4 2.0 %copy-start.11 = (f32[8,512]{1,0:T(8,128)S(1)}, f32[8,512]{1,0:T(8,128)}, u32[]{:S(2)}) copy-start(f32[8,512]{1,0:T(8,128)} %get-tuple-element.49) | copy-start | bytes 49156
  54.4 1.8 %copy-start.4 = (f32[8,64]{1,0:T(8,128)S(1)}, f32[8,64]{1,0:T(8,128)}, u32[]{:S(2)}) copy-start(f32[8,64]{1,0:T(8,128)} %get-tuple-element.50) | copy-start | bytes 6148
  54.4 1.8 %copy-start.5 = (f32[8,64]{1,0:T(8,128)S(1)}, f32[8,64]{1,0:T(8,128)}, u32[]{:S(2)}) copy-start(f32[8,64]{1,0:T(8,128)} %get-tuple-element.51) | copy-start | bytes 6148
  55.1 1.9 %copy-start.3 = (f32[1,4,16,128]{3,2,1,0:T(8,128)S(1)}, f32[1,4,16,128]{3,2,1,0:T(8,128)}, u32[]{:S(2)}) copy-start(f32[1,4,16,128]{3,2,1,0:T(8,128)} %get-tuple-element.36) | copy-start | bytes 98308
  63.1 1.8 %copy-start.2 = (bf16[1,4,2048]{2,1,0:T(4,128)(2,1)S(1)}, bf16[1,4,2048]{2,1,0:T(4,128)(2,1)}, u32[]{:S(2)}) copy-start(bf16[1,4,2048]{2,1,0:T(4,128)(2,1)} %copy-done.1) | copy-start | bytes 49156
  63.1 1.8 %copy-start.20 = (f32[4]{0:T(128)S(1)}, f32[4]{0:T(128)}, u32[]{:S(2)}) copy-start(f32[4]{0:T(128)} %dynamic_slice.7) | copy-start | bytes 52
  63.7 1.6 %copy-start.13 = (f32[3,4]{1,0:T(4,128)S(1)}, f32[3,4]{1,0:T(4,128)}, u32[]{:S(2)}) copy-start(f32[3,4]{1,0:T(4,128)} %copy-done.12) | copy-start | bytes 148
  63.8 1.6 %copy-start.15 = (f32[3,4]{1,0:T(4,128)S(1)}, f32[3,4]{1,0:T(4,128)}, u32[]{:S(2)}) copy-start(f32[3,4]{1,0:T(4,128)} %copy-done.14) | copy-start | bytes 148
  63.8 1.6 %copy-start.17 = (f32[3,4,1]{1,0,2:T(4,128)S(1)}, f32[3,4,1]{1,0,2:T(4,128)}, u32[]{:S(2)}) copy-start(f32[3,4,1]{1,0,2:T(4,128)} %copy-done.16) | copy-start | bytes 148
  63.8 10.2 %copy-start.19 = (f32[4]{0:T(128)S(1)}, f32[4]{0:T(128)}, u32[]{:S(2)}) copy-start(f32[4]{0:T(128)} %get-tuple-element.7) | copy-start | bytes 52
  70.5 37.2 %all-to-all-start.2 = ((bf16[8,2,5,4,128]{4,1,3,2,0:T(2,128)(2,1)}), bf16[8,2,5,4,128]{4,1,3,2,0:T(2,128)(2,1)S(1)}, u32[]{:S(2)}, u32[]{:S(2)}) async-start(bf16[8,2,5,4,128]{4,1,3,2,0:T(2,128)(2,1)} %copy.145), calls=%async_computation.2 | async-start | bytes 163840 | tf_op jit(solution)/shard_map/all_to_all | solution.py:32
where the time goes:
time: 110 us
  blocking collectives  36.1 us (33%)
  local copies, waits for them, and re-layouts  32.6 us (30%)
  starting transfers between devices  20.8 us (19%)
  matrix products  7.48 us (7%)
  waiting for transfers between devices  6.38 us (6%)
  other arithmetic  4.81 us (4%)
  between operations  1.52 us (1%)
    all_gather x1, blocking collectives, gather_turned(): result, at, done = (lax.all_gather(both, axis, axis=0, tiled=True), 0, [])  32 us
    all_to_all x1, starting transfers between devices, shards(): lax.all_to_all(stacked, SEQ, split_axis=1, concat_axis=2, tiled=True)  17.4 us
    unnamed x55, local copies, waits for them, and re-layouts  7.83 us
    all_to_all x1, waiting for transfers between devices, shards(): lax.all_to_all(stacked, SEQ, split_axis=1, concat_axis=2, tiled=True)  6.38 us
    dot_general x16, matrix products, first_axis(): jnp.einsum('...ab,ak->...kb', operand, matrix, precision=lax.Precision.HIGH)  4.38 us
    all_to_all x1, blocking collectives, exchange_in_order(): lax.all_to_all(parts, axes[k], split_axis=k, concat_axis=k, tiled=True)  4.11 us
    reshape x3, local copies, waits for them, and re-layouts, transform(): jnp.swapaxes(inner_imag, -1, -2).reshape(real_part.shape)  3.5 us
    reshape x3, local copies, waits for them, and re-layouts, transform(): jnp.swapaxes(inner_real, -1, -2).reshape(real_part.shape)  3.49 us
  transfers between devices with their start and end apart: 2, of which 1 were waited for; matrix products, arithmetic and copies ran while one was open for 5% of the time, Pallas kernels for 0%

commit v1 on v0

v1 whole, which is shorter than its diff:
```python
import jax
import jax.numpy as jnp
from jax import lax
from jax.experimental import pallas as pl
from jax.experimental.pallas import tpu as pltpu
from jax.sharding import PartitionSpec as P

LANES = 128
ROWS = 24
STREAMS = 5
PIECES = 3

F32 = jnp.float32
BF16 = jnp.bfloat16


def iota(shape, dim):
    return lax.broadcasted_iota(jnp.int32, shape, dim)


def pack_kernel(features, cotangent, long_filter, out, wide, packed, *, groups, per_group):
    channels = groups * per_group
    for i in range(3):
        wide[i * channels : (i + 1) * channels, :] = features[i].astype(F32)
    wide[3 * channels : 4 * channels, :] = cotangent[...].astype(F32)
    wide[4 * channels : 5 * channels, :] = long_filter[...].astype(F32)
    for i in range(STREAMS):
        for c in range(per_group):
            rows = wide[pl.ds(i * channels + c, groups, stride=per_group), :]
            packed[pl.ds(i * per_group + c, groups, stride=ROWS), :] = rows
    for r in range(STREAMS * per_group, ROWS):
        packed[pl.ds(r, groups, stride=ROWS), :] = jnp.zeros((groups, LANES), F32)
    out[...] = packed[...].reshape(groups, ROWS, LANES).astype(BF16)


def shifted_down(values, count):
    if count == 0:
        return values
    size = values.shape[0]
    return jnp.where(iota(values.shape, 0) >= count, pltpu.roll(values, count, 0), 0.0)


def shifted_up(values, count):
    if count == 0:
        return values
    size = values.shape[0]
    return jnp.where(iota(values.shape, 0) < size - count, pltpu.roll(values, size - count, 0), 0.0)


def delayed(values, offset):
    if offset == 0:
        return values
    turned = pltpu.roll(values, offset, 1)
    return jnp.where(iota(values.shape, 1) >= offset, turned, shifted_down(turned, 1))


def advanced(values, offset):
    if offset == 0:
        return values
    turned = pltpu.roll(values, LANES - offset, 1)
    return jnp.where(iota(values.shape, 1) < LANES - offset, turned, shifted_up(turned, 1))


def fill_toeplitz(rows, target):
    square = (LANES, LANES)
    keep = iota(square, 1) >= iota(square, 0)
    before = jnp.zeros(square, F32)
    for k in range(rows.shape[0]):
        line = jnp.broadcast_to(rows[k : k + 1, :], square)
        turned = pltpu.roll(line, 0, 1, stride=1, stride_axis=0)
        target[:, k * LANES : (k + 1) * LANES] = jnp.where(keep, turned, before).astype(BF16)
        before = turned


def middle_kernel(where, weights, gain, received, out, wide, packed, filter_band, mixed_band):
    blocks = received.shape[0]
    per_group = weights.shape[2] // blocks
    taps = weights.shape[1]
    wide[...] = received[...].astype(F32).reshape(blocks * ROWS, LANES)
    first = where[0] * per_group
    sums = []
    for c in range(per_group):

        def stream(i):
            return wide[pl.ds(i * per_group + c, blocks, stride=ROWS), :]

        def put(i, values):
            packed[pl.ds(i * per_group + c, blocks, stride=ROWS), :] = values

        w = [[weights[i, o, first + c] for o in range(taps)] for i in range(3)]
        local_gain = gain[first + c]
        history = [[delayed(stream(i), o) for o in range(taps)] for i in range(3)]
        primed = []
        for i in range(3):
            running = w[i][0] * history[i][0]
            for o in range(1, taps):
                running = running + w[i][o] * history[i][o]
            primed.append(running)
        cot = stream(3)
        mixed = (primed[1] * primed[2]).astype(BF16).astype(F32)
        gated = (cot * primed[0]).astype(BF16).astype(F32)
        fill_toeplitz(stream(4), filter_band)
        fill_toeplitz(mixed, mixed_band)
        spread = jnp.dot(mixed.astype(BF16), filter_band[...], preferred_element_type=F32)
        conv = spread[:, 0:LANES]
        for k in range(1, blocks):
            conv = conv + shifted_down(spread[:, k * LANES : (k + 1) * LANES], k)
        ahead = jnp.concatenate([shifted_up(gated, k).astype(BF16) for k in range(blocks)], axis=1)
        across = (((1,), (1,)), ((), ()))
        corr = lax.dot_general(ahead, filter_band[...], across, preferred_element_type=F32)
        cross = lax.dot_general(ahead, mixed_band[...], across, preferred_element_type=F32)
        long_out = (conv + local_gain * mixed).astype(BF16).astype(F32)
        mixed_grad = (corr + local_gain * gated).astype(BF16).astype(F32)
        primed_grad = [cot * long_out, mixed_grad * primed[2], mixed_grad * primed[1]]
        put(0, primed[0] * long_out)
        for i in range(3):
            running = w[i][0] * primed_grad[i]
            for o in range(1, taps):
                running = running + w[i][o] * advanced(primed_grad[i], o)
            put(1 + i, running)
        put(4, cross)
        for i in range(3):
            for o in range(taps):
                sums.append(jnp.sum(primed_grad[i] * history[i][o], axis=0, keepdims=True))
        sums.append(jnp.sum(gated * mixed, axis=0, keepdims=True))
    count = len(sums)
    totals = jnp.sum(jnp.concatenate(sums, axis=0), axis=1, keepdims=True)
    shape = (count, LANES)
    line = jnp.sum(jnp.where(iota(shape, 0) == iota(shape, 1), totals, 0.0), axis=0, keepdims=True)
    line = jnp.broadcast_to(line, (8, LANES))
    left, row = line, jnp.zeros_like(line)
    for p in range(PIECES):
        piece = left.astype(BF16).astype(F32)
        left = left - piece
        row = row + (pltpu.roll(piece, p * count, 1) if p else piece)
    row = jnp.broadcast_to(row[0:1, :], (blocks, LANES))
    used = STREAMS * per_group
    packed[pl.ds(used, blocks, stride=ROWS), :] = row
    for r in range(used + 1, ROWS):
        packed[pl.ds(r, blocks, stride=ROWS), :] = jnp.zeros((blocks, LANES), F32)
    out[...] = packed[...].reshape(blocks, ROWS, LANES).astype(BF16)


def unpack_kernel(
    received, gated_out, feature_grad, long_grad, short_grad, skip_grad, wide, rows_out, *, per_group
):
    groups = received.shape[0]
    channels = groups * per_group
    wide[...] = received[...].astype(F32).reshape(groups * ROWS, LANES)
    for i in range(STREAMS):
        for c in range(per_group):
            rows = wide[pl.ds(i * per_group + c, groups, stride=ROWS), :]
            rows_out[pl.ds(i * channels + c, groups, stride=per_group), :] = rows
    gated_out[...] = rows_out[0:channels, :].astype(BF16)
    for i in range(3):
        feature_grad[i] = rows_out[(1 + i) * channels : (2 + i) * channels, :].astype(BF16)
    long_grad[...] = rows_out[4 * channels : 5 * channels, :].astype(BF16)
    pieces = wide[pl.ds(STREAMS * per_group, groups, stride=ROWS), :].astype(BF16)
    taps = short_grad.shape[1]
    each = 3 * taps + 1
    shape = (groups, LANES)
    owner = (iota(shape, 1) // per_group == iota(shape, 0)).astype(F32).astype(BF16)
    turned = lax.dot_general(pieces, owner, (((0,), (0,)), ((), ())), preferred_element_type=F32)
    place = iota((each, LANES), 1) % per_group
    total = jnp.zeros((each, LANES), F32)
    for c in range(per_group):
        value = jnp.zeros((each, LANES), F32)
        for p in range(PIECES):
            at = (p * per_group + c) * each
            value = value + turned[at : at + each, :]
        total = jnp.where(place == c, value, total)
    for i in range(3):
        short_grad[i] = total[i * taps : (i + 1) * taps, 0:channels]
    skip_grad[...] = total[3 * taps : 3 * taps + 1, 0:channels]


def vmem(shape, dtype=F32):
    return pltpu.VMEM(shape, dtype)


def solution(mesh):
    groups = mesh.shape["seq"]

    def exchange(parts):
        return lax.all_to_all(parts, "seq", split_axis=0, concat_axis=0, tiled=True)

    def shards(features, cotangent, long_filter, short_filters, skip_gain):
        channels = features.shape[1]
        per_group = channels // groups
        taps = short_filters.shape[2]
        whole = pl.BlockSpec(memory_space=pltpu.VMEM)
        scalars = pl.BlockSpec(memory_space=pltpu.SMEM)
        parts_shape = jax.ShapeDtypeStruct((groups, ROWS, LANES), BF16)
        flat = (groups * ROWS, LANES)
        tall = (STREAMS * channels, LANES)
        parts = pl.pallas_call(
            lambda *refs: pack_kernel(*refs, groups=groups, per_group=per_group),
            name="pack",
            out_shape=parts_shape,
            in_specs=[whole] * 3,
            out_specs=whole,
            scratch_shapes=[vmem(tall), vmem(flat)],
        )(features, cotangent, long_filter)
        columns = exchange(parts)
        where = lax.axis_index("seq").astype(jnp.int32).reshape(1)
        band = (LANES, groups * LANES)
        results = pl.pallas_call(
            middle_kernel,
            name="middle",
            out_shape=parts_shape,
            in_specs=[scalars, scalars, scalars, whole],
            out_specs=whole,
            scratch_shapes=[vmem(flat), vmem(flat), vmem(band, BF16), vmem(band, BF16)],
        )(where, jnp.swapaxes(short_filters, 1, 2), skip_gain, columns)
        back = exchange(results)
        gated_out, feature_grad, long_grad, short_grad, skip_grad = pl.pallas_call(
            lambda *refs: unpack_kernel(*refs, per_group=per_group),
            name="unpack",
            out_shape=(
                jax.ShapeDtypeStruct((channels, LANES), BF16),
                jax.ShapeDtypeStruct((3, channels, LANES), BF16),
                jax.ShapeDtypeStruct((channels, LANES), BF16),
                jax.ShapeDtypeStruct((3, taps, channels), F32),
                jax.ShapeDtypeStruct((1, channels), F32),
            ),
            in_specs=[whole],
            out_specs=(whole,) * 5,
            scratch_shapes=[vmem(flat), vmem(tall)],
        )(back)
        return (
            gated_out,
            feature_grad,
            long_grad,
            jnp.swapaxes(short_grad, 1, 2),
            skip_grad.reshape(channels),
        )

    return jax.shard_map(
        shards,
        mesh=mesh,
        in_specs=(
            P(None, "chan", "seq"),
            P("chan", "seq"),
            P("chan", "seq"),
            P(None, "chan", None),
            P("chan"),
        ),
        out_specs=(
            P("chan", "seq"),
            P(None, "chan", "seq"),
            P("chan", "seq"),
            P(None, "chan", None),
            P("chan"),
        ),
        check_vma=False,
    )
```

time: 110 us -> 50.2 us (0.46)
  local copies, waits for them, and re-layouts: 32.6 us -> 0.64 us
  blocking collectives: 36.1 us -> 14.4 us
  matrix products: 7.48 us -> 0 us
  Pallas kernels: 0 us -> 6.95 us
  other arithmetic: 4.81 us -> 0 us
  waiting for transfers between devices: 6.38 us -> 9.81 us
  starting transfers between devices: 20.8 us -> 17.4 us
    all_gather x1 -> x0, blocking collectives: 32 us -> none  [gather_turned(): result, at, done = (lax.all_gather(both, axis, axis=0, tiled=True), 0, [])]
    all_to_all x1, blocking collectives: 4.11 us -> 14.4 us  [exchange(): return lax.all_to_all(parts, 'seq', split_axis=0, concat_axis=0, tiled=True)]
    reshape x15 -> x0, local copies, waits for them, and re-layouts: 8.3 us -> none  [the longest x3 3.5 us: transform(): jnp.swapaxes(inner_imag, -1, -2).reshape(real_part.shape)]
    dot_general x24 -> x0, matrix products: 7.48 us -> none  [the longest x16 4.38 us: first_axis(): jnp.einsum('...ab,ak->...kb', operand, matrix, precision=lax.Precision.HIGH)]
    unnamed x55 -> x2, local copies, waits for them, and re-layouts: 7.83 us -> 0.64 us
    pallas_call x0 -> x3, Pallas kernels: none -> 6.95 us  [the longest x1 3.75 us: shards(): pl.pallas_call(middle_kernel, name='middle', out_shape=parts_shape, in_sp...]
    slice x16 -> x0, local copies, waits for them, and re-layouts: 4.42 us -> none  [the longest x1 0.89 us: featurize(): running = weights[:, :, 0:1] * history[:, :, margin:margin + span_count]]
    squeeze x6 -> x0, local copies, waits for them, and re-layouts: 3.77 us -> none  [the longest x2 1.68 us: spectral(): packed_real = freq_real[0]]
  transfers between devices with their start and end apart: 2 -> 1, of which waited for: 1 -> 1; matrix products, arithmetic and copies ran while one was open for 5% -> 0% of each run, Pallas kernels for 0% -> 0%
where the time goes in v1:
time: 50.2 us; the launch traced here: 49.8 us
  starting transfers between devices  17.4 us (35%)
  blocking collectives  14.4 us (29%)
  waiting for transfers between devices  9.81 us (20%)
  Pallas kernels  6.95 us (14%)
  local copies, waits for them, and re-layouts  0.64 us (1%)
  between operations  0.64 us (1%)
    all_to_all x1, starting transfers between devices, exchange(): return lax.all_to_all(parts, 'seq', split_axis=0, concat_axis=0, tiled=True)  17.4 us
    all_to_all x1, blocking collectives, exchange(): return lax.all_to_all(parts, 'seq', split_axis=0, concat_axis=0, tiled=True)  14.4 us
    all_to_all x1, waiting for transfers between devices, exchange(): return lax.all_to_all(parts, 'seq', split_axis=0, concat_axis=0, tiled=True)  9.81 us
    pallas_call x1, Pallas kernels, shards(): pl.pallas_call(middle_kernel, name='middle', out_shape=parts_shape, in_sp...  3.75 us
    pallas_call x1, Pallas kernels, shards(): pl.pallas_call(lambda *refs: unpack_kernel(*refs, per_group=per_group), n...  1.71 us
    pallas_call x1, Pallas kernels, shards(): pl.pallas_call(lambda *refs: pack_kernel(*refs, groups=groups, per_group=...  1.5 us
  transfers between devices with their start and end apart: 1, of which 1 were waited for; matrix products, arithmetic and copies ran while one was open for 0% of the time, Pallas kernels for 0%

profile of v1, /device:TPU:1, one launch (start us, length us, event | category | flops | bytes accessed | tf_op | source)
XLA Modules:
  0.0 49.8 jit_solution(15252252822040960697)
XLA Ops:
  0.6 1.5 %pack.1 = bf16[16,24,128]{2,1,0:T(8,128)(2,1)} custom-call(bf16[3,64,128]{2,1,0:T(8,128)(2,1)} %refs_0_.1, bf16[64,128]{1,0:T(8,128)(2,1)} %refs_1_.1, bf16[64,128]{1,0:T(8,128)(2,1)} %refs_2_.1), custom_call_target="tpu_custom_call" | custom-call | tf_op jit(solution)/shard_map/pack/pallas_call | solution.py:196
  2.1 17.4 %all-to-all-start = ((bf16[16,24,128]{2,1,0:T(8,128)(2,1)}), bf16[16,24,128]{2,1,0:T(8,128)(2,1)S(1)}, u32[]{:S(2)}, u32[]{:S(2)}) async-start(bf16[16,24,128]{2,1,0:T(8,128)(2,1)} %pack.1), calls=%async_computation | async-start | bytes 196608 | tf_op jit(solution)/shard_map/all_to_all | solution.py:185
  19.5 9.8 %all-to-all-done.received = bf16[16,24,128]{2,1,0:T(8,128)(2,1)S(1)} async-done(((bf16[16,24,128]{2,1,0:T(8,128)(2,1)}), bf16[16,24,128]{2,1,0:T(8,128)(2,1)S(1)}, u32[]{:S(2)}, u32[]{:S(2)}) %all-to-all-start) | async-done | bytes 98336 | tf_op jit(solution)/shard_map/all_to_all | solution.py:185
  29.4 0.0 copy-start
  29.4 0.6 %copy-done = bf16[16,24,128]{2,1,0:T(8,128)(2,1)} copy-done((bf16[16,24,128]{2,1,0:T(8,128)(2,1)}, bf16[16,24,128]{2,1,0:T(8,128)(2,1)S(1)}, u32[]{:S(2)}) %copy-start) | copy-done | bytes 98328
  30.0 3.7 %middle.1 = bf16[16,24,128]{2,1,0:T(8,128)(2,1)} custom-call(s32[1]{0:T(128)} %bitcast.where, f32[3,3,64]{2,1,0:T(4,128)} %bitcast.4, f32[64]{0:T(128)} %gain.1, bf16[16,24,128]{2,1,0:T(8,128)(2,1)} %copy-done), custom_call_target="tpu_custom_call" | custom-call | tf_op jit(solution)/shard_map/middle/pallas_call | solution.py:207
  33.7 14.4 %all_to_all.10.refs_0_ = bf16[16,24,128]{2,1,0:T(8,128)(2,1)} all-to-all(bf16[16,24,128]{2,1,0:T(8,128)(2,1)} %middle.1), channel_id=1, replica_groups=mesh['seq'=16,'chan'=64] {'seq'}, dimensions={0} | all-to-all | bytes 196608 | tf_op jit(solution)/shard_map/all_to_all | solution.py:185
  48.1 1.7 %unpack.1 = (bf16[64,128]{1,0:T(8,128)(2,1)}, bf16[3,64,128]{2,1,0:T(8,128)(2,1)}, bf16[64,128]{1,0:T(8,128)(2,1)}, f32[3,3,64]{2,1,0:T(4,128)}, f32[1,64]{1,0:T(1,128)}) custom-call(bf16[16,24,128]{2,1,0:T(8,128)(2,1)} %all_to_all.10.refs_0_), custom_call_target="tpu_custom_call" | custom-call | tf_op jit(solution)/shard_map/unpack/pallas_call | solution.py:216
Async XLA Ops:
  2.1 27.2 %all-to-all-start = ((bf16[16,24,128]{2,1,0:T(8,128)(2,1)}), bf16[16,24,128]{2,1,0:T(8,128)(2,1)S(1)}, u32[]{:S(2)}, u32[]{:S(2)}) async-start(bf16[16,24,128]{2,1,0:T(8,128)(2,1)} %pack.1), calls=%async_computation | async-start | bytes 196608 | tf_op jit(solution)/shard_map/all_to_all | solution.py:185
  29.4 0.6 %copy-start = (bf16[16,24,128]{2,1,0:T(8,128)(2,1)}, bf16[16,24,128]{2,1,0:T(8,128)(2,1)S(1)}, u32[]{:S(2)}) copy-start(bf16[16,24,128]{2,1,0:T(8,128)(2,1)S(1)} %all-to-all-done.received) | copy-start | bytes 294916

commit v2 on v1

--- a/solution.py
+++ b/solution.py
@@ -72,12 +72,12 @@
         before = turned
 
 
-def middle_kernel(where, weights, gain, received, out, wide, packed, filter_band, mixed_band):
+def middle_kernel(weights, gain, received, out, wide, packed, filter_band, mixed_band):
     blocks = received.shape[0]
     per_group = weights.shape[2] // blocks
     taps = weights.shape[1]
     wide[...] = received[...].astype(F32).reshape(blocks * ROWS, LANES)
-    first = where[0] * per_group
+    first = lax.axis_index("seq") * per_group
     sums = []
     for c in range(per_group):
 
@@ -196,26 +196,28 @@
         parts = pl.pallas_call(
             lambda *refs: pack_kernel(*refs, groups=groups, per_group=per_group),
             name="pack",
+            compiler_params=pltpu.CompilerParams(vmem_limit_bytes=4 << 20),
             out_shape=parts_shape,
             in_specs=[whole] * 3,
             out_specs=whole,
             scratch_shapes=[vmem(tall), vmem(flat)],
         )(features, cotangent, long_filter)
         columns = exchange(parts)
-        where = lax.axis_index("seq").astype(jnp.int32).reshape(1)
         band = (LANES, groups * LANES)
         results = pl.pallas_call(
             middle_kernel,
             name="middle",
+            compiler_params=pltpu.CompilerParams(vmem_limit_bytes=8 << 20),
             out_shape=parts_shape,
-            in_specs=[scalars, scalars, scalars, whole],
+            in_specs=[scalars, scalars, whole],
             out_specs=whole,
             scratch_shapes=[vmem(flat), vmem(flat), vmem(band, BF16), vmem(band, BF16)],
-        )(where, jnp.swapaxes(short_filters, 1, 2), skip_gain, columns)
+        )(jnp.swapaxes(short_filters, 1, 2), skip_gain, columns)
         back = exchange(results)
         gated_out, feature_grad, long_grad, short_grad, skip_grad = pl.pallas_call(
             lambda *refs: unpack_kernel(*refs, per_group=per_group),
             name="unpack",
+            compiler_params=pltpu.CompilerParams(vmem_limit_bytes=4 << 20),
             out_shape=(
                 jax.ShapeDtypeStruct((channels, LANES), BF16),
                 jax.ShapeDtypeStruct((3, channels, LANES), BF16),

time: 50.2 us -> 46.8 us (0.932)
  blocking collectives: 14.4 us -> 39.1 us
  starting transfers between devices: 17.4 us -> 0 us
  waiting for transfers between devices: 9.81 us -> 0 us
  Pallas kernels: 6.95 us -> 3.72 us
  local copies, waits for them, and re-layouts: 0.64 us -> 2.88 us
    all_to_all x1 -> x2, blocking collectives: 14.4 us -> 39.1 us  [exchange(): return lax.all_to_all(parts, 'seq', split_axis=0, concat_axis=0, tiled=True)]
    all_to_all x1 -> x0, starting transfers between devices: 17.4 us -> none  [exchange(): return lax.all_to_all(parts, 'seq', split_axis=0, concat_axis=0, tiled=True)]
    all_to_all x1 -> x0, waiting for transfers between devices: 9.81 us -> none  [exchange(): return lax.all_to_all(parts, 'seq', split_axis=0, concat_axis=0, tiled=True)]
    unnamed x2 -> x10, local copies, waits for them, and re-layouts: 0.64 us -> 2.88 us
    pallas_call x1, Pallas kernels: 1.5 us -> 0.06 us  [shards(): pl.pallas_call(lambda *refs: pack_kernel(*refs, groups=groups, per_group=...]
    pallas_call x1, Pallas kernels: 3.75 us -> 2.85 us  [shards(): pl.pallas_call(middle_kernel, name='middle', compiler_params=pltpu.Compil...]
    pallas_call x1, Pallas kernels: 1.71 us -> 0.82 us  [shards(): pl.pallas_call(lambda *refs: unpack_kernel(*refs, per_group=per_group), n...]
  transfers between devices with their start and end apart: 1 -> 0, of which waited for: 1 -> 0; matrix products, arithmetic and copies ran while one was open for 0% -> 0% of each run, Pallas kernels for 0% -> 0%
where the time goes in v2:
time: 46.8 us; the launch traced here: 46.4 us
  blocking collectives  39.1 us (84%)
  Pallas kernels  3.72 us (8%)
  local copies, waits for them, and re-layouts  2.88 us (6%)
  between operations  0.66 us (1%)
    all_to_all x2, blocking collectives, exchange(): return lax.all_to_all(parts, 'seq', split_axis=0, concat_axis=0, tiled=True)  39.1 us
    unnamed x10, local copies, waits for them, and re-layouts  2.88 us
    pallas_call x1, Pallas kernels, shards(): pl.pallas_call(middle_kernel, name='middle', compiler_params=pltpu.Compil...  2.85 us

profile of v2, /device:TPU:1, one launch (start us, length us, event | category | flops | bytes accessed | tf_op | source)
XLA Modules:
  0.0 46.4 jit_solution(7218891980021294669)
XLA Ops:
  0.6 0.0 copy-start
  0.6 0.8 %copy-done = bf16[3,64,128]{2,1,0:T(8,128)(2,1)S(1)} copy-done((bf16[3,64,128]{2,1,0:T(8,128)(2,1)S(1)}, bf16[3,64,128]{2,1,0:T(8,128)(2,1)}, u32[]{:S(2)}) %copy-start) | copy-done | bytes 49176
  1.4 0.0 copy-start.1
  1.4 0.7 %copy-done.1 = bf16[64,128]{1,0:T(8,128)(2,1)S(1)} copy-done((bf16[64,128]{1,0:T(8,128)(2,1)S(1)}, bf16[64,128]{1,0:T(8,128)(2,1)}, u32[]{:S(2)}) %copy-start.1) | copy-done | bytes 16408
  2.1 0.0 copy-start.2
  2.2 0.7 %copy-done.2 = bf16[64,128]{1,0:T(8,128)(2,1)S(1)} copy-done((bf16[64,128]{1,0:T(8,128)(2,1)S(1)}, bf16[64,128]{1,0:T(8,128)(2,1)}, u32[]{:S(2)}) %copy-start.2) | copy-done | bytes 16408
  2.9 0.1 pack.1
  2.9 0.0 copy-start.3
  2.9 26.3 %all_to_all.10.received = bf16[16,24,128]{2,1,0:T(8,128)(2,1)S(1)} all-to-all(bf16[16,24,128]{2,1,0:T(8,128)(2,1)S(1)} %pack.1), channel_id=1, replica_groups=mesh['seq'=16,'chan'=64] {'seq'}, dimensions={0} | all-to-all | bytes 196608 | tf_op jit(solution)/shard_map/all_to_all | solution.py:185
  29.3 0.0 copy-start.4
  29.3 0.0 copy-done.3
  29.3 0.7 %copy-done.4 = f32[64]{0:T(128)S(1)} copy-done((f32[64]{0:T(128)S(1)}, f32[64]{0:T(128)}, u32[]{:S(2)}) %copy-start.4) | copy-done | bytes 280
  29.9 2.9 %middle.1 = bf16[16,24,128]{2,1,0:T(8,128)(2,1)S(1)} custom-call(f32[3,3,64]{2,1,0:T(4,128)S(1)} %bitcast.3, f32[64]{0:T(128)S(1)} %copy-done.4, bf16[16,24,128]{2,1,0:T(8,128)(2,1)S(1)} %all_to_all.10.received), custom_call_target="tpu_custom_call" | custom-call | tf_op jit(solution)/shard_map/middle/pallas_call | solution.py:207
  32.8 12.8 %all_to_all.11.refs_0_ = bf16[16,24,128]{2,1,0:T(8,128)(2,1)S(1)} all-to-all(bf16[16,24,128]{2,1,0:T(8,128)(2,1)S(1)} %middle.1), channel_id=1, replica_groups=mesh['seq'=16,'chan'=64] {'seq'}, dimensions={0} | all-to-all | bytes 196608 | tf_op jit(solution)/shard_map/all_to_all | solution.py:185
  45.6 0.8 %unpack.1 = (bf16[64,128]{1,0:T(8,128)(2,1)}, bf16[3,64,128]{2,1,0:T(8,128)(2,1)}, bf16[64,128]{1,0:T(8,128)(2,1)}, f32[3,3,64]{2,1,0:T(4,128)}, f32[1,64]{1,0:T(1,128)}) custom-call(bf16[16,24,128]{2,1,0:T(8,128)(2,1)S(1)} %all_to_all.11.refs_0_), custom_call_target="tpu_custom_call" | custom-call | tf_op jit(solution)/shard_map/unpack/pallas_call | solution.py:217
Async XLA Ops:
  0.6 0.8 %copy-start = (bf16[3,64,128]{2,1,0:T(8,128)(2,1)S(1)}, bf16[3,64,128]{2,1,0:T(8,128)(2,1)}, u32[]{:S(2)}) copy-start(bf16[3,64,128]{2,1,0:T(8,128)(2,1)} %refs_0_.1) | copy-start | bytes 147460
  1.4 0.7 %copy-start.1 = (bf16[64,128]{1,0:T(8,128)(2,1)S(1)}, bf16[64,128]{1,0:T(8,128)(2,1)}, u32[]{:S(2)}) copy-start(bf16[64,128]{1,0:T(8,128)(2,1)} %refs_1_.1) | copy-start | bytes 49156
  2.1 0.7 %copy-start.2 = (bf16[64,128]{1,0:T(8,128)(2,1)S(1)}, bf16[64,128]{1,0:T(8,128)(2,1)}, u32[]{:S(2)}) copy-start(bf16[64,128]{1,0:T(8,128)(2,1)} %refs_2_.1) | copy-start | bytes 49156
  2.9 26.3 %copy-start.3 = (f32[3,64,3]{1,2,0:T(4,128)S(1)}, f32[3,64,3]{1,2,0:T(4,128)}, u32[]{:S(2)}) copy-start(f32[3,64,3]{1,2,0:T(4,128)} %param.8) | copy-start | bytes 6916
  29.3 0.7 %copy-start.4 = (f32[64]{0:T(128)S(1)}, f32[64]{0:T(128)}, u32[]{:S(2)}) copy-start(f32[64]{0:T(128)} %gain.1) | copy-start | bytes 772

commit v3 on v1

v3 whole, which is shorter than its diff:
```python
import jax
import jax.numpy as jnp
from jax import lax
from jax.experimental import pallas as pl
from jax.experimental.pallas import tpu as pltpu
from jax.sharding import Mesh
from jax.sharding import PartitionSpec as P

SEQ = ("x", "y", "c")
SIDES = (4, 2, 2)
OWNERS = ("x", "c")
BLOCKS = 16
GROUPS = 8
EACH = 8
LANES = 128
STREAMS = 5
TAPS = 3
SUMS = 3 * TAPS + 1
PIECES = 3
IN_ROWS = STREAMS * EACH
OUT_ROWS = IN_ROWS + 8
PHASES = 4
STEP = LANES // PHASES

F32 = jnp.float32
BF16 = jnp.bfloat16


def iota(shape, dim):
    return lax.broadcasted_iota(jnp.int32, shape, dim)


def pack_kernel(features, cotangent, long_filter, weights, gain, out, table, taps, gains, sems):
    small = [
        pltpu.make_async_copy(weights, taps, sems.at[0]),
        pltpu.make_async_copy(gain, gains, sems.at[1]),
    ]
    sources = [features.at[i] for i in range(3)] + [cotangent, long_filter]
    large = []
    for i, source in enumerate(sources):
        for y in range(SIDES[1]):
            target = out.at[:, y, :, pl.ds(i * EACH, EACH), :]
            large.append(pltpu.make_async_copy(source, target, sems.at[2 + 2 * i + y]))
    for copy in small + large:
        copy.start()
    for copy in small:
        copy.wait()
    first = (lax.axis_index("x") * SIDES[2] + lax.axis_index("c")) * EACH
    channels = gains.shape[1]
    shape = (EACH, channels)
    chosen = iota(shape, 1) == iota(shape, 0) + first
    for j in range(SUMS):
        line = gains[...] if j == 3 * TAPS else taps[j // TAPS, j % TAPS : j % TAPS + 1, :]
        line = jnp.broadcast_to(line, shape)
        column = jnp.sum(jnp.where(chosen, line, 0.0), axis=1, keepdims=True)
        table[j] = jnp.broadcast_to(column, (EACH, LANES))
    for copy in large:
        copy.wait()


def shifted_down(values, count):
    if count == 0:
        return values
    return jnp.where(iota(values.shape, 0) >= count, pltpu.roll(values, count, 0), 0.0)


def shifted_up(values, count):
    if count == 0:
        return values
    size = values.shape[0]
    return jnp.where(iota(values.shape, 0) < size - count, pltpu.roll(values, size - count, 0), 0.0)


def later(values, count, carry):
    if count == 0:
        return values
    turned = pltpu.roll(values, count, 1)
    return jnp.where(iota(values.shape, 1) >= count, turned, carry(turned, 1))


def earlier(values, count):
    if count == 0:
        return values
    turned = pltpu.roll(values, LANES - count, 1)
    return jnp.where(iota(values.shape, 1) < LANES - count, turned, shifted_up(turned, 1))


def fill_right(line_of, right, column):
    shape = (STEP, LANES)
    keep = iota(shape, 1) >= iota(shape, 0)
    before = jnp.zeros(shape, F32)
    for k in range(BLOCKS):
        line = jnp.broadcast_to(line_of(k), shape)
        turned = pltpu.roll(line, 0, 1, stride=1, stride_axis=0)
        part = jnp.where(keep, turned, before).astype(BF16)
        right[k * STEP : (k + 1) * STEP, column : column + LANES] = part
        before = turned


def left_rows(values, shifted):
    turned = [pltpu.roll(values, STEP * q, 1) if q else values for q in range(PHASES)]
    moved = [[shifted(turned[q], kk) for q in range(PHASES)] for kk in range(PHASES)]
    part = iota(values.shape, 1) // STEP
    rows = []
    for p in range(PHASES):
        base = moved[0][-p % PHASES]
        for kk in range(1, PHASES):
            base = jnp.where(part == kk, moved[kk][(kk - p) % PHASES], base)
        tiles = [shifted(base, PHASES * j).astype(BF16) for j in range(BLOCKS // PHASES)]
        rows.append(jnp.concatenate(tiles, axis=1))
    return rows


def joined(parts, carry):
    total = parts[0]
    for p in range(1, PHASES):
        total = total + later(parts[p], STEP * p, carry)
    return total


def middle_kernel(table, received, out, wide, packed, right, kept, mirrored, turned_back):
    wide[...] = received[...].astype(F32).reshape(BLOCKS * IN_ROWS, LANES)
    square = (LANES, LANES)
    mirror = jnp.where(iota(square, 0) + iota(square, 1) == LANES - 1, 1.0, 0.0).astype(BF16)

    def stream(i, c):
        return wide[pl.ds(i * EACH + c, BLOCKS, stride=IN_ROWS), :]

    def put(i, c, values):
        packed[pl.ds(i * EACH + c, BLOCKS, stride=OUT_ROWS), :] = values

    def weight(j, c):
        return table[j, c : c + 1, :]

    def rows(c):
        return slice(c * BLOCKS, (c + 1) * BLOCKS)

    PRIMED, MIXED, GATED, HISTORY, LONG = 0, 3, 4, 5, 11
    for c in range(EACH):
        primed = []
        for i in range(3):
            value = stream(i, c)
            running = weight(i * TAPS, c) * value
            for o in range(1, TAPS):
                moved = later(value, o, shifted_down)
                kept[HISTORY + 2 * i + o - 1, rows(c), :] = moved
                running = running + weight(i * TAPS + o, c) * moved
            kept[PRIMED + i, rows(c), :] = running
            primed.append(running)
        kept[MIXED, rows(c), :] = (primed[1] * primed[2]).astype(BF16).astype(F32)
        kept[GATED, rows(c), :] = (stream(3, c) * primed[0]).astype(BF16).astype(F32)
    mirrored[...] = jnp.dot(kept[GATED].astype(BF16), mirror, preferred_element_type=F32)
    half = EACH * BLOCKS
    for c in range(EACH):
        gain = weight(3 * TAPS, c)
        mixed = kept[MIXED, rows(c), :]
        gated = mirrored[rows(c), :]
        fill_right(lambda k: wide[k * IN_ROWS + 4 * EACH + c : k * IN_ROWS + 4 * EACH + c + 1, :], right.at[c], 0)
        fill_right(lambda k: kept[MIXED, c * BLOCKS + k : c * BLOCKS + k + 1, :], right.at[c], LANES)
        left = jnp.concatenate(left_rows(mixed, shifted_down) + left_rows(gated, shifted_up), axis=0)
        product = jnp.dot(left, right[c], preferred_element_type=F32)

        def parts(at, column):
            cut = slice(column, column + LANES)
            return [product[at + p * BLOCKS : at + (p + 1) * BLOCKS, cut] for p in range(PHASES)]

        conv = joined(parts(0, 0), shifted_down)
        corr = joined(parts(PHASES * BLOCKS, 0), shifted_up)
        cross = joined(parts(PHASES * BLOCKS, LANES), shifted_up)
        kept[LONG, rows(c), :] = (conv + gain * mixed).astype(BF16).astype(F32)
        turned_back[rows(c), :] = corr + gain * gated
        turned_back[half + c * BLOCKS : half + (c + 1) * BLOCKS, :] = cross
    turned_back[...] = jnp.dot(turned_back[...].astype(BF16), mirror, preferred_element_type=F32)
    sums = [[] for _ in range(SUMS)]
    for c in range(EACH):
        cot = stream(3, c)
        primed = [kept[PRIMED + i, rows(c), :] for i in range(3)]
        long_out = kept[LONG, rows(c), :]
        mixed_grad = turned_back[rows(c), :]
        primed_grad = [cot * long_out, mixed_grad * primed[2], mixed_grad * primed[1]]
        put(0, c, primed[0] * long_out)
        put(4, c, turned_back[half + c * BLOCKS : half + (c + 1) * BLOCKS, :])
        for i in range(3):
            running = weight(i * TAPS, c) * primed_grad[i]
            for o in range(1, TAPS):
                running = running + weight(i * TAPS + o, c) * earlier(primed_grad[i], o)
            put(1 + i, c, running)
            for o in range(TAPS):
                past = kept[HISTORY + 2 * i + o - 1, rows(c), :] if o else stream(i, c)
                sums[i * TAPS + o].append(jnp.sum(primed_grad[i] * past, axis=0, keepdims=True))
        both = kept[GATED, rows(c), :] * kept[MIXED, rows(c), :]
        sums[3 * TAPS].append(jnp.sum(both, axis=0, keepdims=True))
    stacked = jnp.concatenate([line for lines in sums for line in lines], axis=0)
    totals = jnp.sum(stacked, axis=1, keepdims=True)
    shape = stacked.shape
    line = jnp.sum(jnp.where(iota(shape, 0) == iota(shape, 1), totals, 0.0), axis=0, keepdims=True)
    left = jnp.broadcast_to(line, (BLOCKS, LANES))
    for r in range(IN_ROWS, OUT_ROWS):
        piece = left.astype(BF16).astype(F32)
        if r >= IN_ROWS + PIECES:
            piece = jnp.zeros_like(piece)
        left = left - piece
        packed[pl.ds(r, BLOCKS, stride=OUT_ROWS), :] = piece
    side = lax.axis_index("y")
    wanted = SIDES[2] * OUT_ROWS
    for x in range(SIDES[0]):
        at = pl.multiple_of((SIDES[1] * x + side) * wanted, 8)
        block = packed[pl.ds(at, wanted), :].astype(BF16)
        out[SIDES[2] * x : SIDES[2] * (x + 1)] = block.reshape(SIDES[2], OUT_ROWS, LANES)


def unpack_kernel(
    received, gated_out, feature_grad, long_grad, short_grad, skip_grad, taps, gains, sems
):
    targets = [gated_out] + [feature_grad.at[i] for i in range(3)] + [long_grad]
    copies = []
    for i, target in enumerate(targets):
        source = received.at[:, pl.ds(i * EACH, EACH), :]
        copies.append(pltpu.make_async_copy(source, target, sems.at[i]))
        copies[-1].start()
    pieces = received[:, IN_ROWS:OUT_ROWS, :].astype(F32)
    shape = (GROUPS, LANES)
    owner = jnp.where(iota(shape, 1) // EACH == iota(shape, 0), 1.0, 0.0).astype(BF16)
    total = jnp.zeros((LANES, LANES), F32)
    for p in range(PIECES):
        piece = pieces[:, p, :].astype(BF16)
        total = total + lax.dot_general(
            piece, owner, (((0,), (0,)), ((), ())), preferred_element_type=F32
        )
    total = total[: SUMS * EACH, :].reshape(SUMS, EACH, LANES)
    mine = iota(total.shape, 1) == iota(total.shape, 2) % EACH
    lines = jnp.sum(jnp.where(mine, total, 0.0), axis=1)
    channels = gains.shape[1]
    for i in range(3):
        taps[i] = lines[i * TAPS : (i + 1) * TAPS, 0:channels]
    gains[...] = lines[3 * TAPS :, 0:channels]
    last = [
        pltpu.make_async_copy(taps, short_grad, sems.at[STREAMS]),
        pltpu.make_async_copy(gains, skip_grad, sems.at[STREAMS + 1]),
    ]
    for copy in last:
        copy.start()
    for copy in copies + last:
        copy.wait()


def grant(mebibytes):
    return pltpu.CompilerParams(vmem_limit_bytes=mebibytes << 20)


def shards(features, cotangent, long_filter, short_filters, skip_gain):
    channels = features.shape[1]
    whole = pl.BlockSpec(memory_space=pltpu.VMEM)
    far = pl.BlockSpec(memory_space=pltpu.HBM)
    cut = (SIDES[0], SIDES[2], EACH, LANES)
    parts, table = pl.pallas_call(
        pack_kernel,
        name="pack",
        compiler_params=grant(4),
        out_shape=(
            jax.ShapeDtypeStruct((*SIDES, IN_ROWS, LANES), BF16),
            jax.ShapeDtypeStruct((SUMS, EACH, LANES), F32),
        ),
        in_specs=[far] * 5,
        out_specs=(whole, whole),
        scratch_shapes=[
            pltpu.VMEM((3, TAPS, channels), F32),
            pltpu.VMEM((1, channels), F32),
            pltpu.SemaphoreType.DMA((2 + 2 * STREAMS,)),
        ],
    )(
        features.reshape(3, *cut),
        cotangent.reshape(cut),
        long_filter.reshape(cut),
        jnp.swapaxes(short_filters, 1, 2),
        skip_gain.reshape(1, channels),
    )
    columns = lax.all_to_all(
        parts.reshape(BLOCKS, IN_ROWS, LANES), SEQ, split_axis=0, concat_axis=0, tiled=True
    )
    results = pl.pallas_call(
        middle_kernel,
        name="middle",
        compiler_params=grant(12),
        out_shape=jax.ShapeDtypeStruct((GROUPS, OUT_ROWS, LANES), BF16),
        in_specs=[whole, whole],
        out_specs=whole,
        scratch_shapes=[
            pltpu.VMEM((BLOCKS * IN_ROWS, LANES), F32),
            pltpu.VMEM((BLOCKS * OUT_ROWS, LANES), F32),
            pltpu.VMEM((EACH, BLOCKS * STEP, 2 * LANES), BF16),
            pltpu.VMEM((12, EACH * BLOCKS, LANES), F32),
            pltpu.VMEM((EACH * BLOCKS, LANES), F32),
            pltpu.VMEM((2 * EACH * BLOCKS, LANES), F32),
        ],
    )(table, columns)
    back = lax.all_to_all(results, OWNERS, split_axis=0, concat_axis=0, tiled=True)
    block = (GROUPS, EACH, LANES)
    gated_out, feature_grad, long_grad, short_grad, skip_grad = pl.pallas_call(
        unpack_kernel,
        name="unpack",
        compiler_params=grant(4),
        out_shape=(
            jax.ShapeDtypeStruct(block, BF16),
            jax.ShapeDtypeStruct((3, *block), BF16),
            jax.ShapeDtypeStruct(block, BF16),
            jax.ShapeDtypeStruct((3, TAPS, channels), F32),
            jax.ShapeDtypeStruct((1, channels), F32),
        ),
        in_specs=[whole],
        out_specs=(far,) * 5,
        scratch_shapes=[
            pltpu.VMEM((3, TAPS, channels), F32),
            pltpu.VMEM((1, channels), F32),
            pltpu.SemaphoreType.DMA((STREAMS + 2,)),
        ],
    )(back)
    return (
        gated_out.reshape(channels, LANES),
        feature_grad.reshape(3, channels, LANES),
        long_grad.reshape(channels, LANES),
        jnp.swapaxes(short_grad, 1, 2),
        skip_grad.reshape(channels),
    )


def solution(mesh):
    torus = Mesh(mesh.devices.reshape(*SIDES, mesh.shape["chan"]), (*SEQ, "chan"))
    return jax.shard_map(
        shards,
        mesh=torus,
        in_specs=(
            P(None, "chan", SEQ),
            P("chan", SEQ),
            P("chan", SEQ),
            P(None, "chan", None),
            P("chan"),
        ),
        out_specs=(
            P("chan", SEQ),
            P(None, "chan", SEQ),
            P("chan", SEQ),
            P(None, "chan", None),
            P("chan"),
        ),
        check_vma=False,
    )
```

time: 50.2 us -> 42.2 us (0.84)
  blocking collectives: 14.4 us -> 35 us
  starting transfers between devices: 17.4 us -> 0 us
  waiting for transfers between devices: 9.81 us -> 0 us
  Pallas kernels: 6.95 us -> 3.23 us
  local copies, waits for them, and re-layouts: 0.64 us -> 2.91 us
    all_to_all x1 -> x2, blocking collectives: 14.4 us -> 35 us  [the longest x1 26.9 us: shards(): lax.all_to_all(parts.reshape(BLOCKS, IN_ROWS, LANES), SEQ, split_axis=0,...]
    all_to_all x1 -> x0, starting transfers between devices: 17.4 us -> none  [exchange(): return lax.all_to_all(parts, 'seq', split_axis=0, concat_axis=0, tiled=True)]
    all_to_all x1 -> x0, waiting for transfers between devices: 9.81 us -> none  [exchange(): return lax.all_to_all(parts, 'seq', split_axis=0, concat_axis=0, tiled=True)]
    pallas_call x3, Pallas kernels: 6.95 us -> 3.23 us  [the longest x1 2.1 us: shards(): pl.pallas_call(middle_kernel, name='middle', compiler_params=grant(12), o...]
    unnamed x2 -> x10, local copies, waits for them, and re-layouts: 0.64 us -> 2.91 us
  transfers between devices with their start and end apart: 1 -> 0, of which waited for: 1 -> 0; matrix products, arithmetic and copies ran while one was open for 0% -> 0% of each run, Pallas kernels for 0% -> 0%
where the time goes in v3:
time: 42.2 us; the launch traced here: 41.8 us
  blocking collectives  35 us (83%)
  Pallas kernels  3.23 us (8%)
  local copies, waits for them, and re-layouts  2.91 us (7%)
  between operations  0.67 us (2%)
    all_to_all x1, blocking collectives, shards(): lax.all_to_all(parts.reshape(BLOCKS, IN_ROWS, LANES), SEQ, split_axis=0,...  26.9 us
    all_to_all x1, blocking collectives, shards(): lax.all_to_all(results, OWNERS, split_axis=0, concat_axis=0, tiled=True)  8.11 us
    unnamed x10, local copies, waits for them, and re-layouts  2.91 us
    pallas_call x1, Pallas kernels, shards(): pl.pallas_call(middle_kernel, name='middle', compiler_params=grant(12), o...  2.1 us
    pallas_call x1, Pallas kernels, shards(): pl.pallas_call(unpack_kernel, name='unpack', compiler_params=grant(4), ou...  0.88 us

profile of v3, /device:TPU:1, one launch (start us, length us, event | category | flops | bytes accessed | tf_op | source)
XLA Modules:
  0.0 41.8 jit_solution(3803251942716943574)
XLA Ops:
  0.6 0.0 copy-start.3
  0.6 0.0 copy-start.4
  0.7 0.7 %copy-done.3 = f32[3,64,3]{1,2,0:T(4,128)S(1)} copy-done((f32[3,64,3]{1,2,0:T(4,128)S(1)}, f32[3,64,3]{1,2,0:T(4,128)}, u32[]{:S(2)}) %copy-start.3) | copy-done | bytes 2328
  1.3 0.0 copy-done.4
  1.3 0.0 copy-start
  1.3 0.8 %copy-done = bf16[3,64,128]{2,1,0:T(8,128)(2,1)S(1)} copy-done((bf16[3,64,128]{2,1,0:T(8,128)(2,1)S(1)}, bf16[3,64,128]{2,1,0:T(8,128)(2,1)}, u32[]{:S(2)}) %copy-start) | copy-done | bytes 49176
  2.1 0.0 copy-start.1
  2.1 0.7 %copy-done.1 = bf16[64,128]{1,0:T(8,128)(2,1)S(1)} copy-done((bf16[64,128]{1,0:T(8,128)(2,1)S(1)}, bf16[64,128]{1,0:T(8,128)(2,1)}, u32[]{:S(2)}) %copy-start.1) | copy-done | bytes 16408
  2.8 0.0 copy-start.2
  2.8 0.7 %copy-done.2 = bf16[64,128]{1,0:T(8,128)(2,1)S(1)} copy-done((bf16[64,128]{1,0:T(8,128)(2,1)S(1)}, bf16[64,128]{1,0:T(8,128)(2,1)}, u32[]{:S(2)}) %copy-start.2) | copy-done | bytes 16408
  3.6 0.3 pack.1
  3.8 26.9 %all_to_all.10.received = bf16[16,40,128]{2,1,0:T(8,128)(2,1)S(1)} all-to-all(bf16[16,40,128]{2,1,0:T(8,128)(2,1)S(1)} %bitcast.11), channel_id=1, replica_groups=mesh['x'=4,'y'=2,'c'=2,'chan'=64] {'x','y','c'}, dimensions={0} | all-to-all | bytes 327680 | tf_op jit(solution)/shard_map/all_to_all | solution.py:278
  30.7 2.1 %middle.1 = bf16[8,48,128]{2,1,0:T(8,128)(2,1)S(1)} custom-call(f32[10,8,128]{2,1,0:T(8,128)S(1)} %get-tuple-element.12.table, bf16[16,40,128]{2,1,0:T(8,128)(2,1)S(1)} %all_to_all.10.received), custom_call_target="tpu_custom_call" | custom-call | tf_op jit(solution)/shard_map/middle/pallas_call | solution.py:281
  32.8 8.1 %all_to_all.11.received = bf16[8,48,128]{2,1,0:T(8,128)(2,1)S(1)} all-to-all(bf16[8,48,128]{2,1,0:T(8,128)(2,1)S(1)} %middle.1), channel_id=1, replica_groups=mesh['x'=4,'y'=2,'c'=2,'chan'=64] {'x','c'}, dimensions={0} | all-to-all | bytes 196608 | tf_op jit(solution)/shard_map/all_to_all | solution.py:297
  40.9 0.9 %unpack.1 = (bf16[8,8,128]{2,1,0:T(8,128)(2,1)}, bf16[3,8,8,128]{3,2,1,0:T(8,128)(2,1)}, bf16[8,8,128]{2,1,0:T(8,128)(2,1)}, f32[3,3,64]{2,1,0:T(4,128)}, f32[1,64]{1,0:T(1,128)}) custom-call(bf16[8,48,128]{2,1,0:T(8,128)(2,1)S(1)} %all_to_all.11.received), custom_call_target="tpu_custom_call" | custom-call | tf_op jit(solution)/shard_map/unpack/pallas_call | solution.py:299
Async XLA Ops:
  0.6 0.7 %copy-start.3 = (f32[3,64,3]{1,2,0:T(4,128)S(1)}, f32[3,64,3]{1,2,0:T(4,128)}, u32[]{:S(2)}) copy-start(f32[3,64,3]{1,2,0:T(4,128)} %param.8) | copy-start | bytes 6916
  0.6 0.7 %copy-start.4 = (f32[64]{0:T(128)S(1)}, f32[64]{0:T(128)}, u32[]{:S(2)}) copy-start(f32[64]{0:T(128)} %param.9) | copy-start | bytes 772
  1.3 0.8 %copy-start = (bf16[3,64,128]{2,1,0:T(8,128)(2,1)S(1)}, bf16[3,64,128]{2,1,0:T(8,128)(2,1)}, u32[]{:S(2)}) copy-start(bf16[3,64,128]{2,1,0:T(8,128)(2,1)} %param.5) | copy-start | bytes 147460
  2.1 0.7 %copy-start.1 = (bf16[64,128]{1,0:T(8,128)(2,1)S(1)}, bf16[64,128]{1,0:T(8,128)(2,1)}, u32[]{:S(2)}) copy-start(bf16[64,128]{1,0:T(8,128)(2,1)} %param.6) | copy-start | bytes 49156
  2.8 0.7 %copy-start.2 = (bf16[64,128]{1,0:T(8,128)(2,1)S(1)}, bf16[64,128]{1,0:T(8,128)(2,1)}, u32[]{:S(2)}) copy-start(bf16[64,128]{1,0:T(8,128)(2,1)} %param.7) | copy-start | bytes 49156

commit v4 on v3

--- a/solution.py
+++ b/solution.py
@@ -248,6 +248,10 @@
     return pltpu.CompilerParams(vmem_limit_bytes=mebibytes << 20)
 
 
+def stay(array):
+    return pltpu.with_memory_space_constraint(array, pltpu.HBM)
+
+
 def shards(features, cotangent, long_filter, short_filters, skip_gain):
     channels = features.shape[1]
     whole = pl.BlockSpec(memory_space=pltpu.VMEM)
@@ -269,11 +273,11 @@
             pltpu.SemaphoreType.DMA((2 + 2 * STREAMS,)),
         ],
     )(
-        features.reshape(3, *cut),
-        cotangent.reshape(cut),
-        long_filter.reshape(cut),
-        jnp.swapaxes(short_filters, 1, 2),
-        skip_gain.reshape(1, channels),
+        stay(features.reshape(3, *cut)),
+        stay(cotangent.reshape(cut)),
+        stay(long_filter.reshape(cut)),
+        stay(jnp.swapaxes(short_filters, 1, 2)),
+        stay(skip_gain.reshape(1, channels)),
     )
     columns = lax.all_to_all(
         parts.reshape(BLOCKS, IN_ROWS, LANES), SEQ, split_axis=0, concat_axis=0, tiled=True

time: 42.2 us -> 39.9 us (0.945)
  local copies, waits for them, and re-layouts: 2.91 us -> 0 us
  Pallas kernels: 3.23 us -> 3.98 us
    unnamed x10 -> x0, local copies, waits for them, and re-layouts: 2.91 us -> none
    pallas_call x1, Pallas kernels: 0.25 us -> 1 us  [shards(): pl.pallas_call(pack_kernel, name='pack', compiler_params=grant(4), out_sh...]
where the time goes in v4:
time: 39.9 us; the launch traced here: 39.6 us
  blocking collectives  35 us (88%)
  Pallas kernels  3.98 us (10%)
  between operations  0.65 us (2%)
    all_to_all x1, blocking collectives, shards(): lax.all_to_all(parts.reshape(BLOCKS, IN_ROWS, LANES), SEQ, split_axis=0,...  26.9 us
    all_to_all x1, blocking collectives, shards(): lax.all_to_all(results, OWNERS, split_axis=0, concat_axis=0, tiled=True)  8.11 us
    pallas_call x1, Pallas kernels, shards(): pl.pallas_call(middle_kernel, name='middle', compiler_params=grant(12), o...  2.1 us
    pallas_call x1, Pallas kernels, shards(): pl.pallas_call(pack_kernel, name='pack', compiler_params=grant(4), out_sh...  1 us
    pallas_call x1, Pallas kernels, shards(): pl.pallas_call(unpack_kernel, name='unpack', compiler_params=grant(4), ou...  0.88 us

profile of v4, /device:TPU:1, one launch (start us, length us, event | category | flops | bytes accessed | tf_op | source)
XLA Modules:
  0.0 39.6 jit_solution(11976248308426632912)
XLA Ops:
  0.6 1.0 %pack.1 = (bf16[4,2,2,40,128]{4,3,2,1,0:T(8,128)(2,1)S(1)}, f32[10,8,128]{2,1,0:T(8,128)S(1)}) custom-call(bf16[3,4,2,8,128]{4,3,2,1,0:T(8,128)(2,1)} %bitcast.12, bf16[4,2,8,128]{3,2,1,0:T(8,128)(2,1)} %bitcast.13, bf16[4,2,8,128]{3,2,1,0:T(8,128)(2,1)} %bitcast.14, f32[3,3,64]{2,1,0:T(4,128)} %bitcast.15, f32[1,64]{1,0:T(1,128)} %bitcast.16), custom_call_target="tpu_custom_call" | custom-call | tf_op jit(solution)/shard_map/pack/pallas_call | solution.py:260
  1.6 26.9 %all_to_all.10.received = bf16[16,40,128]{2,1,0:T(8,128)(2,1)S(1)} all-to-all(bf16[16,40,128]{2,1,0:T(8,128)(2,1)S(1)} %bitcast.11), channel_id=1, replica_groups=mesh['x'=4,'y'=2,'c'=2,'chan'=64] {'x','y','c'}, dimensions={0} | all-to-all | bytes 327680 | tf_op jit(solution)/shard_map/all_to_all | solution.py:282
  28.5 2.1 %middle.1 = bf16[8,48,128]{2,1,0:T(8,128)(2,1)S(1)} custom-call(f32[10,8,128]{2,1,0:T(8,128)S(1)} %get-tuple-element.12.table, bf16[16,40,128]{2,1,0:T(8,128)(2,1)S(1)} %all_to_all.10.received), custom_call_target="tpu_custom_call" | custom-call | tf_op jit(solution)/shard_map/middle/pallas_call | solution.py:285
  30.6 8.1 %all_to_all.11.received = bf16[8,48,128]{2,1,0:T(8,128)(2,1)S(1)} all-to-all(bf16[8,48,128]{2,1,0:T(8,128)(2,1)S(1)} %middle.1), channel_id=1, replica_groups=mesh['x'=4,'y'=2,'c'=2,'chan'=64] {'x','c'}, dimensions={0} | all-to-all | bytes 196608 | tf_op jit(solution)/shard_map/all_to_all | solution.py:301
  38.7 0.9 %unpack.1 = (bf16[8,8,128]{2,1,0:T(8,128)(2,1)}, bf16[3,8,8,128]{3,2,1,0:T(8,128)(2,1)}, bf16[8,8,128]{2,1,0:T(8,128)(2,1)}, f32[3,3,64]{2,1,0:T(4,128)}, f32[1,64]{1,0:T(1,128)}) custom-call(bf16[8,48,128]{2,1,0:T(8,128)(2,1)S(1)} %all_to_all.11.received), custom_call_target="tpu_custom_call" | custom-call | tf_op jit(solution)/shard_map/unpack/pallas_call | solution.py:303

commit v5 on v4

--- a/solution.py
+++ b/solution.py
@@ -16,11 +16,13 @@
 STREAMS = 5
 TAPS = 3
 SUMS = 3 * TAPS + 1
-PIECES = 3
 IN_ROWS = STREAMS * EACH
-OUT_ROWS = IN_ROWS + 8
+OUT_ROWS = IN_ROWS + 16
 PHASES = 4
 STEP = LANES // PHASES
+PAD = 8
+BUFFERS = 8
+SPLIT = 8
 
 F32 = jnp.float32
 BF16 = jnp.bfloat16
@@ -58,34 +60,17 @@
         copy.wait()
 
 
-def shifted_down(values, count):
-    if count == 0:
-        return values
-    return jnp.where(iota(values.shape, 0) >= count, pltpu.roll(values, count, 0), 0.0)
-
-
-def shifted_up(values, count):
-    if count == 0:
-        return values
-    size = values.shape[0]
-    return jnp.where(iota(values.shape, 0) < size - count, pltpu.roll(values, size - count, 0), 0.0)
-
-
-def later(values, count, carry):
-    if count == 0:
-        return values
-    turned = pltpu.roll(values, count, 1)
-    return jnp.where(iota(values.shape, 1) >= count, turned, carry(turned, 1))
-
-
-def earlier(values, count):
-    if count == 0:
-        return values
-    turned = pltpu.roll(values, LANES - count, 1)
-    return jnp.where(iota(values.shape, 1) < LANES - count, turned, shifted_up(turned, 1))
-
-
-def fill_right(line_of, right, column):
+def after(values, before, count):
+    mixed = jnp.where(iota(values.shape, 1) < LANES - count, values, before)
+    return pltpu.roll(mixed, count, 1)
+
+
+def ahead(values, behind, count):
+    mixed = jnp.where(iota(values.shape, 1) >= count, values, behind)
+    return pltpu.roll(mixed, LANES - count, 1)
+
+
+def fill_right(line_of, right):
     shape = (STEP, LANES)
     keep = iota(shape, 1) >= iota(shape, 0)
     before = jnp.zeros(shape, F32)
@@ -93,84 +78,150 @@
         line = jnp.broadcast_to(line_of(k), shape)
         turned = pltpu.roll(line, 0, 1, stride=1, stride_axis=0)
         part = jnp.where(keep, turned, before).astype(BF16)
-        right[k * STEP : (k + 1) * STEP, column : column + LANES] = part
+        right[k * STEP : (k + 1) * STEP, :] = part
         before = turned
 
 
-def left_rows(values, shifted):
-    turned = [pltpu.roll(values, STEP * q, 1) if q else values for q in range(PHASES)]
-    moved = [[shifted(turned[q], kk) for q in range(PHASES)] for kk in range(PHASES)]
+class Slide:
+    def __init__(self, ref, down):
+        self.ref, self.down = ref, down
+
+    def clear(self):
+        at = 0 if self.down else BLOCKS
+        self.ref[at : at + PAD, :] = jnp.zeros((PAD, LANES), F32)
+
+    def put(self, values):
+        at = PAD if self.down else 0
+        self.ref[at : at + BLOCKS, :] = values
+
+    def read(self, count):
+        at = PAD - count if self.down else count
+        return self.ref[at : at + BLOCKS, :]
+
+
+def left_rows(values, turned, based):
+    for q in range(PHASES):
+        turned[q].put(pltpu.roll(values, STEP * q, 1) if q else values)
+    moved = [[turned[q].read(kk) for q in range(PHASES)] for kk in range(PHASES)]
     part = iota(values.shape, 1) // STEP
+    zero = jnp.zeros((PAD, LANES), F32)
     rows = []
     for p in range(PHASES):
         base = moved[0][-p % PHASES]
         for kk in range(1, PHASES):
             base = jnp.where(part == kk, moved[kk][(kk - p) % PHASES], base)
-        tiles = [shifted(base, PHASES * j).astype(BF16) for j in range(BLOCKS // PHASES)]
-        rows.append(jnp.concatenate(tiles, axis=1))
+        based[p].put(base)
+        tiles = [base, based[p].read(PHASES)]
+        for tile in tiles[:2]:
+            if based[p].down:
+                tiles.append(jnp.concatenate([zero, tile[:PAD]], axis=0))
+            else:
+                tiles.append(jnp.concatenate([tile[PAD:], zero], axis=0))
+        rows.append(jnp.concatenate([tile.astype(BF16) for tile in tiles], axis=1))
     return rows
 
 
-def joined(parts, carry):
+def joined(parts, slides):
     total = parts[0]
     for p in range(1, PHASES):
-        total = total + later(parts[p], STEP * p, carry)
+        slides[p - 1].put(parts[p])
+        total = total + after(parts[p], slides[p - 1].read(1), STEP * p)
     return total
 
 
-def middle_kernel(table, received, out, wide, packed, right, kept, mirrored, turned_back):
-    wide[...] = received[...].astype(F32).reshape(BLOCKS * IN_ROWS, LANES)
+def middle_kernel(
+    table, received, out, wide, packed, right, kept, mirrored, turned_back, turn, base, piece, grad
+):
+    pad = jnp.zeros((IN_ROWS, LANES), F32)
+    wide[0:IN_ROWS, :] = pad
+    wide[(BLOCKS + 1) * IN_ROWS : (BLOCKS + 2) * IN_ROWS, :] = pad
+    wide[IN_ROWS : (BLOCKS + 1) * IN_ROWS, :] = (
+        received[...].astype(F32).reshape(BLOCKS * IN_ROWS, LANES)
+    )
     square = (LANES, LANES)
     mirror = jnp.where(iota(square, 0) + iota(square, 1) == LANES - 1, 1.0, 0.0).astype(BF16)
 
-    def stream(i, c):
-        return wide[pl.ds(i * EACH + c, BLOCKS, stride=IN_ROWS), :]
+    def stream(i, c, back=0):
+        at = (1 - back) * IN_ROWS + i * EACH + c
+        return wide[pl.ds(at, BLOCKS, stride=IN_ROWS), :]
 
     def put(i, c, values):
-        packed[pl.ds(i * EACH + c, BLOCKS, stride=OUT_ROWS), :] = values
+        packed[pl.ds(i * EACH + c, BLOCKS, stride=IN_ROWS), :] = values
 
     def weight(j, c):
         return table[j, c : c + 1, :]
 
     def rows(c):
         return slice(c * BLOCKS, (c + 1) * BLOCKS)
+
+    def slides(ref, buffer, down):
+        return [Slide(ref.at[buffer, n], d) for n, d in enumerate(down)]
+
+    signals = [True] * PHASES + [False] * PHASES
+    pieces = [True] * (PHASES - 1) + [False] * (2 * (PHASES - 1))
+    turns = [slides(turn, n, signals) for n in range(BUFFERS)]
+    bases = [slides(base, n, signals) for n in range(BUFFERS)]
+    splits = [slides(piece, n, pieces) for n in range(BUFFERS)]
+    grads = [slides(grad, n, [False] * 3) for n in range(BUFFERS)]
+    for group in (turns, bases, splits, grads):
+        for line in group:
+            for slide in line:
+                slide.clear()
 
     PRIMED, MIXED, GATED, HISTORY, LONG = 0, 3, 4, 5, 11
     for c in range(EACH):
         primed = []
         for i in range(3):
-            value = stream(i, c)
+            value, before = stream(i, c), stream(i, c, 1)
             running = weight(i * TAPS, c) * value
             for o in range(1, TAPS):
-                moved = later(value, o, shifted_down)
+                moved = after(value, before, o)
                 kept[HISTORY + 2 * i + o - 1, rows(c), :] = moved
                 running = running + weight(i * TAPS + o, c) * moved
             kept[PRIMED + i, rows(c), :] = running
             primed.append(running)
         kept[MIXED, rows(c), :] = (primed[1] * primed[2]).astype(BF16).astype(F32)
         kept[GATED, rows(c), :] = (stream(3, c) * primed[0]).astype(BF16).astype(F32)
-    mirrored[...] = jnp.dot(kept[GATED].astype(BF16), mirror, preferred_element_type=F32)
     half = EACH * BLOCKS
+    for n in range(SPLIT):
+        cut = slice(n * half // SPLIT, (n + 1) * half // SPLIT)
+        turned = jnp.dot(kept[GATED, cut, :].astype(BF16), mirror, preferred_element_type=F32)
+        mirrored[cut, :] = turned
     for c in range(EACH):
         gain = weight(3 * TAPS, c)
         mixed = kept[MIXED, rows(c), :]
         gated = mirrored[rows(c), :]
-        fill_right(lambda k: wide[k * IN_ROWS + 4 * EACH + c : k * IN_ROWS + 4 * EACH + c + 1, :], right.at[c], 0)
-        fill_right(lambda k: kept[MIXED, c * BLOCKS + k : c * BLOCKS + k + 1, :], right.at[c], LANES)
-        left = jnp.concatenate(left_rows(mixed, shifted_down) + left_rows(gated, shifted_up), axis=0)
-        product = jnp.dot(left, right[c], preferred_element_type=F32)
-
-        def parts(at, column):
+        at = IN_ROWS + 4 * EACH + c
+        fill_right(lambda k: wide[at + k * IN_ROWS : at + k * IN_ROWS + 1, :], right.at[c, 0])
+        fill_right(
+            lambda k: kept[MIXED, c * BLOCKS + k : c * BLOCKS + k + 1, :], right.at[c, 1]
+        )
+        turned, based, split = turns[c % BUFFERS], bases[c % BUFFERS], splits[c % BUFFERS]
+        left = left_rows(mixed, turned[:PHASES], based[:PHASES])
+        left += left_rows(gated, turned[PHASES:], based[PHASES:])
+        product = jnp.dot(
+            jnp.concatenate(left, axis=0),
+            jnp.concatenate([right[c, 0], right[c, 1]], axis=1),
+            preferred_element_type=F32,
+        )
+
+        def parts(first, column):
             cut = slice(column, column + LANES)
-            return [product[at + p * BLOCKS : at + (p + 1) * BLOCKS, cut] for p in range(PHASES)]
-
-        conv = joined(parts(0, 0), shifted_down)
-        corr = joined(parts(PHASES * BLOCKS, 0), shifted_up)
-        cross = joined(parts(PHASES * BLOCKS, LANES), shifted_up)
+            lines = [first + p * BLOCKS for p in range(PHASES)]
+            return [product[line : line + BLOCKS, cut] for line in lines]
+
+        each = PHASES - 1
+        conv = joined(parts(0, 0), split[:each])
+        corr = joined(parts(PHASES * BLOCKS, 0), split[each : 2 * each])
+        cross = joined(parts(PHASES * BLOCKS, LANES), split[2 * each :])
         kept[LONG, rows(c), :] = (conv + gain * mixed).astype(BF16).astype(F32)
         turned_back[rows(c), :] = corr + gain * gated
         turned_back[half + c * BLOCKS : half + (c + 1) * BLOCKS, :] = cross
-    turned_back[...] = jnp.dot(turned_back[...].astype(BF16), mirror, preferred_element_type=F32)
+    for n in range(SPLIT):
+        for start in (0, half):
+            cut = slice(start + n * half // SPLIT, start + (n + 1) * half // SPLIT)
+            lines = turned_back[cut, :].astype(BF16)
+            turned_back[cut, :] = jnp.dot(lines, mirror, preferred_element_type=F32)
     sums = [[] for _ in range(SUMS)]
     for c in range(EACH):
         cot = stream(3, c)
@@ -181,9 +232,12 @@
         put(0, c, primed[0] * long_out)
         put(4, c, turned_back[half + c * BLOCKS : half + (c + 1) * BLOCKS, :])
         for i in range(3):
+            slide = grads[c % BUFFERS][i]
+            slide.put(primed_grad[i])
+            behind = slide.read(1)
             running = weight(i * TAPS, c) * primed_grad[i]
             for o in range(1, TAPS):
-                running = running + weight(i * TAPS + o, c) * earlier(primed_grad[i], o)
+                running = running + weight(i * TAPS + o, c) * ahead(primed_grad[i], behind, o)
             put(1 + i, c, running)
             for o in range(TAPS):
                 past = kept[HISTORY + 2 * i + o - 1, rows(c), :] if o else stream(i, c)
@@ -192,21 +246,27 @@
         sums[3 * TAPS].append(jnp.sum(both, axis=0, keepdims=True))
     stacked = jnp.concatenate([line for lines in sums for line in lines], axis=0)
     totals = jnp.sum(stacked, axis=1, keepdims=True)
-    shape = stacked.shape
-    line = jnp.sum(jnp.where(iota(shape, 0) == iota(shape, 1), totals, 0.0), axis=0, keepdims=True)
-    left = jnp.broadcast_to(line, (BLOCKS, LANES))
-    for r in range(IN_ROWS, OUT_ROWS):
-        piece = left.astype(BF16).astype(F32)
-        if r >= IN_ROWS + PIECES:
-            piece = jnp.zeros_like(piece)
-        left = left - piece
-        packed[pl.ds(r, BLOCKS, stride=OUT_ROWS), :] = piece
+    upper = totals.astype(BF16).astype(F32)
+    shape = (SUMS, EACH, LANES)
+    upper = jnp.broadcast_to(upper, stacked.shape).reshape(shape)
+    totals = jnp.broadcast_to(totals, stacked.shape).reshape(shape)
+    channels = GROUPS * EACH
+    lane = iota(shape, 2)
+    first = (lax.axis_index("x") * SIDES[2] + lax.axis_index("c")) * EACH
+    both = jnp.where(lane < channels, upper, totals - upper)
+    mine = lane % channels == iota(shape, 1) + first
+    lines = jnp.sum(jnp.where(mine, both, 0.0), axis=1)
+    rest = jnp.zeros((OUT_ROWS - IN_ROWS - SUMS, LANES), F32)
+    lines = jnp.concatenate([lines, rest], axis=0).astype(BF16)
     side = lax.axis_index("y")
-    wanted = SIDES[2] * OUT_ROWS
+    wanted = SIDES[2] * IN_ROWS
     for x in range(SIDES[0]):
         at = pl.multiple_of((SIDES[1] * x + side) * wanted, 8)
         block = packed[pl.ds(at, wanted), :].astype(BF16)
-        out[SIDES[2] * x : SIDES[2] * (x + 1)] = block.reshape(SIDES[2], OUT_ROWS, LANES)
+        target = slice(SIDES[2] * x, SIDES[2] * (x + 1))
+        out[target, 0:IN_ROWS, :] = block.reshape(SIDES[2], IN_ROWS, LANES)
+    for n in range(GROUPS):
+        out[n, IN_ROWS:OUT_ROWS, :] = lines
 
 
 def unpack_kernel(
@@ -218,22 +278,12 @@
         source = received.at[:, pl.ds(i * EACH, EACH), :]
         copies.append(pltpu.make_async_copy(source, target, sems.at[i]))
         copies[-1].start()
-    pieces = received[:, IN_ROWS:OUT_ROWS, :].astype(F32)
-    shape = (GROUPS, LANES)
-    owner = jnp.where(iota(shape, 1) // EACH == iota(shape, 0), 1.0, 0.0).astype(BF16)
-    total = jnp.zeros((LANES, LANES), F32)
-    for p in range(PIECES):
-        piece = pieces[:, p, :].astype(BF16)
-        total = total + lax.dot_general(
-            piece, owner, (((0,), (0,)), ((), ())), preferred_element_type=F32
-        )
-    total = total[: SUMS * EACH, :].reshape(SUMS, EACH, LANES)
-    mine = iota(total.shape, 1) == iota(total.shape, 2) % EACH
-    lines = jnp.sum(jnp.where(mine, total, 0.0), axis=1)
+    lines = jnp.sum(received[:, IN_ROWS:OUT_ROWS, :].astype(F32), axis=0)
+    lines = lines + pltpu.roll(lines, LANES // 2, 1)
     channels = gains.shape[1]
     for i in range(3):
         taps[i] = lines[i * TAPS : (i + 1) * TAPS, 0:channels]
-    gains[...] = lines[3 * TAPS :, 0:channels]
+    gains[...] = lines[3 * TAPS : SUMS, 0:channels]
     last = [
         pltpu.make_async_copy(taps, short_grad, sems.at[STREAMS]),
         pltpu.make_async_copy(gains, skip_grad, sems.at[STREAMS + 1]),
@@ -290,12 +340,16 @@
         in_specs=[whole, whole],
         out_specs=whole,
         scratch_shapes=[
+            pltpu.VMEM(((BLOCKS + 2) * IN_ROWS, LANES), F32),
             pltpu.VMEM((BLOCKS * IN_ROWS, LANES), F32),
-            pltpu.VMEM((BLOCKS * OUT_ROWS, LANES), F32),
-            pltpu.VMEM((EACH, BLOCKS * STEP, 2 * LANES), BF16),
+            pltpu.VMEM((EACH, 2, BLOCKS * STEP, LANES), BF16),
             pltpu.VMEM((12, EACH * BLOCKS, LANES), F32),
             pltpu.VMEM((EACH * BLOCKS, LANES), F32),
             pltpu.VMEM((2 * EACH * BLOCKS, LANES), F32),
+            pltpu.VMEM((BUFFERS, 2 * PHASES, BLOCKS + PAD, LANES), F32),
+            pltpu.VMEM((BUFFERS, 2 * PHASES, BLOCKS + PAD, LANES), F32),
+            pltpu.VMEM((BUFFERS, 3 * (PHASES - 1), BLOCKS + PAD, LANES), F32),
+            pltpu.VMEM((BUFFERS, 3, BLOCKS + PAD, LANES), F32),
         ],
     )(table, columns)
     back = lax.all_to_all(results, OWNERS, split_axis=0, concat_axis=0, tiled=True)

time: 39.9 us -> 39.9 us (level)
  no operation moved by 1% of the time
where the time goes in v5:
time: 39.9 us; the launch traced here: 39.7 us
  blocking collectives  35.1 us (88%)
  Pallas kernels  3.93 us (10%)
  between operations  0.65 us (2%)
    all_to_all x1, blocking collectives, shards(): lax.all_to_all(parts.reshape(BLOCKS, IN_ROWS, LANES), SEQ, split_axis=0,...  26.9 us
    all_to_all x1, blocking collectives, shards(): lax.all_to_all(results, OWNERS, split_axis=0, concat_axis=0, tiled=True)  8.22 us
    pallas_call x1, Pallas kernels, shards(): pl.pallas_call(middle_kernel, name='middle', compiler_params=grant(12), o...  2.2 us
    pallas_call x1, Pallas kernels, shards(): pl.pallas_call(pack_kernel, name='pack', compiler_params=grant(4), out_sh...  1 us

profile of v5, /device:TPU:1, one launch (start us, length us, event | category | flops | bytes accessed | tf_op | source)
XLA Modules:
  0.0 39.7 jit_solution(15834889231263543099)
XLA Ops:
  0.6 1.0 %pack.1 = (bf16[4,2,2,40,128]{4,3,2,1,0:T(8,128)(2,1)S(1)}, f32[10,8,128]{2,1,0:T(8,128)S(1)}) custom-call(bf16[3,4,2,8,128]{4,3,2,1,0:T(8,128)(2,1)} %bitcast.12, bf16[4,2,8,128]{3,2,1,0:T(8,128)(2,1)} %bitcast.13, bf16[4,2,8,128]{3,2,1,0:T(8,128)(2,1)} %bitcast.14, f32[3,3,64]{2,1,0:T(4,128)} %bitcast.15, f32[1,64]{1,0:T(1,128)} %bitcast.16), custom_call_target="tpu_custom_call" | custom-call | tf_op jit(solution)/shard_map/pack/pallas_call | solution.py:310
  1.6 26.9 %all_to_all.10.received = bf16[16,40,128]{2,1,0:T(8,128)(2,1)S(1)} all-to-all(bf16[16,40,128]{2,1,0:T(8,128)(2,1)S(1)} %bitcast.11), channel_id=1, replica_groups=mesh['x'=4,'y'=2,'c'=2,'chan'=64] {'x','y','c'}, dimensions={0} | all-to-all | bytes 327680 | tf_op jit(solution)/shard_map/all_to_all | solution.py:332
  28.5 2.2 %middle.1 = bf16[8,56,128]{2,1,0:T(8,128)(2,1)S(1)} custom-call(f32[10,8,128]{2,1,0:T(8,128)S(1)} %get-tuple-element.12.table, bf16[16,40,128]{2,1,0:T(8,128)(2,1)S(1)} %all_to_all.10.received), custom_call_target="tpu_custom_call" | custom-call | tf_op jit(solution)/shard_map/middle/pallas_call | solution.py:335
  30.7 8.2 %all_to_all.11.received = bf16[8,56,128]{2,1,0:T(8,128)(2,1)S(1)} all-to-all(bf16[8,56,128]{2,1,0:T(8,128)(2,1)S(1)} %middle.1), channel_id=1, replica_groups=mesh['x'=4,'y'=2,'c'=2,'chan'=64] {'x','c'}, dimensions={0} | all-to-all | bytes 229376 | tf_op jit(solution)/shard_map/all_to_all | solution.py:355
  38.9 0.7 %unpack.1 = (bf16[8,8,128]{2,1,0:T(8,128)(2,1)}, bf16[3,8,8,128]{3,2,1,0:T(8,128)(2,1)}, bf16[8,8,128]{2,1,0:T(8,128)(2,1)}, f32[3,3,64]{2,1,0:T(4,128)}, f32[1,64]{1,0:T(1,128)}) custom-call(bf16[8,56,128]{2,1,0:T(8,128)(2,1)S(1)} %all_to_all.11.received), custom_call_target="tpu_custom_call" | custom-call | tf_op jit(solution)/shard_map/unpack/pallas_call | solution.py:357

commit v6 on v5

--- a/solution.py
+++ b/solution.py
@@ -20,9 +20,6 @@
 OUT_ROWS = IN_ROWS + 16
 PHASES = 4
 STEP = LANES // PHASES
-PAD = 8
-BUFFERS = 8
-SPLIT = 8
 
 F32 = jnp.float32
 BF16 = jnp.bfloat16
@@ -82,55 +79,55 @@
         before = turned
 
 
-class Slide:
-    def __init__(self, ref, down):
-        self.ref, self.down = ref, down
-
-    def clear(self):
-        at = 0 if self.down else BLOCKS
-        self.ref[at : at + PAD, :] = jnp.zeros((PAD, LANES), F32)
-
-    def put(self, values):
-        at = PAD if self.down else 0
-        self.ref[at : at + BLOCKS, :] = values
-
-    def read(self, count):
-        at = PAD - count if self.down else count
-        return self.ref[at : at + BLOCKS, :]
-
-
-def left_rows(values, turned, based):
-    for q in range(PHASES):
-        turned[q].put(pltpu.roll(values, STEP * q, 1) if q else values)
-    moved = [[turned[q].read(kk) for q in range(PHASES)] for kk in range(PHASES)]
+def shifted_down(values, count):
+    if count == 0:
+        return values
+    whole, rest = divmod(count, 8)
+    parts = [values[n : n + 8] for n in range(0, values.shape[0], 8)]
+    zero = jnp.zeros_like(parts[0])
+    if rest:
+        keep = iota(zero.shape, 0) >= rest
+        turned = [pltpu.roll(part, rest, 0) for part in parts]
+        parts = [jnp.where(keep, t, b) for t, b in zip(turned, [zero] + turned[:-1])]
+    return jnp.concatenate([zero] * whole + parts[: len(parts) - whole], axis=0)
+
+
+def shifted_up(values, count):
+    if count == 0:
+        return values
+    whole, rest = divmod(count, 8)
+    parts = [values[n : n + 8] for n in range(0, values.shape[0], 8)]
+    zero = jnp.zeros_like(parts[0])
+    if rest:
+        keep = iota(zero.shape, 0) < 8 - rest
+        turned = [pltpu.roll(part, 8 - rest, 0) for part in parts]
+        parts = [jnp.where(keep, t, b) for t, b in zip(turned, turned[1:] + [zero])]
+    return jnp.concatenate(parts[whole:] + [zero] * whole, axis=0)
+
+
+def left_rows(values, shifted):
+    turned = [pltpu.roll(values, STEP * q, 1) if q else values for q in range(PHASES)]
+    moved = [[shifted(turned[q], kk) for q in range(PHASES)] for kk in range(PHASES)]
     part = iota(values.shape, 1) // STEP
-    zero = jnp.zeros((PAD, LANES), F32)
     rows = []
     for p in range(PHASES):
         base = moved[0][-p % PHASES]
         for kk in range(1, PHASES):
             base = jnp.where(part == kk, moved[kk][(kk - p) % PHASES], base)
-        based[p].put(base)
-        tiles = [base, based[p].read(PHASES)]
-        for tile in tiles[:2]:
-            if based[p].down:
-                tiles.append(jnp.concatenate([zero, tile[:PAD]], axis=0))
-            else:
-                tiles.append(jnp.concatenate([tile[PAD:], zero], axis=0))
-        rows.append(jnp.concatenate([tile.astype(BF16) for tile in tiles], axis=1))
+        tiles = [shifted(base, PHASES * j).astype(BF16) for j in range(BLOCKS // PHASES)]
+        rows.append(jnp.concatenate(tiles, axis=1))
     return rows
 
 
-def joined(parts, slides):
+def joined(parts, shifted):
     total = parts[0]
     for p in range(1, PHASES):
-        slides[p - 1].put(parts[p])
-        total = total + after(parts[p], slides[p - 1].read(1), STEP * p)
+        total = total + after(parts[p], shifted(parts[p], 1), STEP * p)
     return total
 
 
 def middle_kernel(
-    table, received, out, wide, packed, right, kept, mirrored, turned_back, turn, base, piece, grad
+    table, received, out, wide, packed, right, kept, mirrored, turned_back, left, product
 ):
     pad = jnp.zeros((IN_ROWS, LANES), F32)
     wide[0:IN_ROWS, :] = pad
@@ -154,22 +151,11 @@
     def rows(c):
         return slice(c * BLOCKS, (c + 1) * BLOCKS)
 
-    def slides(ref, buffer, down):
-        return [Slide(ref.at[buffer, n], d) for n, d in enumerate(down)]
-
-    signals = [True] * PHASES + [False] * PHASES
-    pieces = [True] * (PHASES - 1) + [False] * (2 * (PHASES - 1))
-    turns = [slides(turn, n, signals) for n in range(BUFFERS)]
-    bases = [slides(base, n, signals) for n in range(BUFFERS)]
-    splits = [slides(piece, n, pieces) for n in range(BUFFERS)]
-    grads = [slides(grad, n, [False] * 3) for n in range(BUFFERS)]
-    for group in (turns, bases, splits, grads):
-        for line in group:
-            for slide in line:
-                slide.clear()
-
     PRIMED, MIXED, GATED, HISTORY, LONG = 0, 3, 4, 5, 11
-    for c in range(EACH):
+    half = EACH * BLOCKS
+    sums = [[] for _ in range(SUMS)]
+
+    def prime(c):
         primed = []
         for i in range(3):
             value, before = stream(i, c), stream(i, c, 1)
@@ -182,48 +168,53 @@
             primed.append(running)
         kept[MIXED, rows(c), :] = (primed[1] * primed[2]).astype(BF16).astype(F32)
         kept[GATED, rows(c), :] = (stream(3, c) * primed[0]).astype(BF16).astype(F32)
-    half = EACH * BLOCKS
-    for n in range(SPLIT):
-        cut = slice(n * half // SPLIT, (n + 1) * half // SPLIT)
-        turned = jnp.dot(kept[GATED, cut, :].astype(BF16), mirror, preferred_element_type=F32)
-        mirrored[cut, :] = turned
-    for c in range(EACH):
-        gain = weight(3 * TAPS, c)
-        mixed = kept[MIXED, rows(c), :]
-        gated = mirrored[rows(c), :]
+
+    def reflect(ref, start, values):
+        ref[start : start + BLOCKS, :] = jnp.dot(
+            values.astype(BF16), mirror, preferred_element_type=F32
+        )
+
+    def filter_band(c):
         at = IN_ROWS + 4 * EACH + c
         fill_right(lambda k: wide[at + k * IN_ROWS : at + k * IN_ROWS + 1, :], right.at[c, 0])
-        fill_right(
-            lambda k: kept[MIXED, c * BLOCKS + k : c * BLOCKS + k + 1, :], right.at[c, 1]
-        )
-        turned, based, split = turns[c % BUFFERS], bases[c % BUFFERS], splits[c % BUFFERS]
-        left = left_rows(mixed, turned[:PHASES], based[:PHASES])
-        left += left_rows(gated, turned[PHASES:], based[PHASES:])
-        product = jnp.dot(
-            jnp.concatenate(left, axis=0),
-            jnp.concatenate([right[c, 0], right[c, 1]], axis=1),
-            preferred_element_type=F32,
-        )
-
-        def parts(first, column):
-            cut = slice(column, column + LANES)
-            lines = [first + p * BLOCKS for p in range(PHASES)]
-            return [product[line : line + BLOCKS, cut] for line in lines]
-
-        each = PHASES - 1
-        conv = joined(parts(0, 0), split[:each])
-        corr = joined(parts(PHASES * BLOCKS, 0), split[each : 2 * each])
-        cross = joined(parts(PHASES * BLOCKS, LANES), split[2 * each :])
-        kept[LONG, rows(c), :] = (conv + gain * mixed).astype(BF16).astype(F32)
-        turned_back[rows(c), :] = corr + gain * gated
+
+    def mixed_band(c):
+        at = c * BLOCKS
+        fill_right(lambda k: kept[MIXED, at + k : at + k + 1, :], right.at[c, 1])
+
+    def turn(c):
+        reflect(mirrored, c * BLOCKS, kept[GATED, rows(c), :])
+
+    def mixed_rows(c):
+        lines = left_rows(kept[MIXED, rows(c), :], shifted_down)
+        left[c, 0 : PHASES * BLOCKS, :] = jnp.concatenate(lines, axis=0)
+
+    def gated_rows(c):
+        lines = left_rows(mirrored[rows(c), :], shifted_up)
+        left[c, PHASES * BLOCKS :, :] = jnp.concatenate(lines, axis=0)
+
+    def multiply(c):
+        band = jnp.concatenate([right[c, 0], right[c, 1]], axis=1)
+        product[c] = jnp.dot(left[c], band, preferred_element_type=F32)
+
+    def parts(c, first, column):
+        lines = [first + p * BLOCKS for p in range(PHASES)]
+        return [product[c, n : n + BLOCKS, column : column + LANES] for n in lines]
+
+    def gather(c):
+        gain = weight(3 * TAPS, c)
+        conv = joined(parts(c, 0, 0), shifted_down)
+        corr = joined(parts(c, PHASES * BLOCKS, 0), shifted_up)
+        cross = joined(parts(c, PHASES * BLOCKS, LANES), shifted_up)
+        kept[LONG, rows(c), :] = (conv + gain * kept[MIXED, rows(c), :]).astype(BF16).astype(F32)
+        turned_back[rows(c), :] = corr + gain * mirrored[rows(c), :]
         turned_back[half + c * BLOCKS : half + (c + 1) * BLOCKS, :] = cross
-    for n in range(SPLIT):
-        for start in (0, half):
-            cut = slice(start + n * half // SPLIT, start + (n + 1) * half // SPLIT)
-            lines = turned_back[cut, :].astype(BF16)
-            turned_back[cut, :] = jnp.dot(lines, mirror, preferred_element_type=F32)
-    sums = [[] for _ in range(SUMS)]
-    for c in range(EACH):
+
+    def turn_back(c):
+        for start in (c * BLOCKS, half + c * BLOCKS):
+            reflect(turned_back, start, turned_back[start : start + BLOCKS, :])
+
+    def finish(c):
         cot = stream(3, c)
         primed = [kept[PRIMED + i, rows(c), :] for i in range(3)]
         long_out = kept[LONG, rows(c), :]
@@ -232,9 +223,7 @@
         put(0, c, primed[0] * long_out)
         put(4, c, turned_back[half + c * BLOCKS : half + (c + 1) * BLOCKS, :])
         for i in range(3):
-            slide = grads[c % BUFFERS][i]
-            slide.put(primed_grad[i])
-            behind = slide.read(1)
+            behind = shifted_up(primed_grad[i], 1)
             running = weight(i * TAPS, c) * primed_grad[i]
             for o in range(1, TAPS):
                 running = running + weight(i * TAPS + o, c) * ahead(primed_grad[i], behind, o)
@@ -244,6 +233,25 @@
                 sums[i * TAPS + o].append(jnp.sum(primed_grad[i] * past, axis=0, keepdims=True))
         both = kept[GATED, rows(c), :] * kept[MIXED, rows(c), :]
         sums[3 * TAPS].append(jnp.sum(both, axis=0, keepdims=True))
+
+    for c in range(EACH):
+        prime(c)
+    for c in range(EACH):
+        turn(c)
+    for c in range(EACH):
+        filter_band(c)
+        mixed_rows(c)
+    for c in range(EACH):
+        mixed_band(c)
+        gated_rows(c)
+    for c in range(EACH):
+        multiply(c)
+    for c in range(EACH):
+        gather(c)
+    for c in range(EACH):
+        turn_back(c)
+    for c in range(EACH):
+        finish(c)
     stacked = jnp.concatenate([line for lines in sums for line in lines], axis=0)
     totals = jnp.sum(stacked, axis=1, keepdims=True)
     upper = totals.astype(BF16).astype(F32)
@@ -346,10 +354,8 @@
             pltpu.VMEM((12, EACH * BLOCKS, LANES), F32),
             pltpu.VMEM((EACH * BLOCKS, LANES), F32),
             pltpu.VMEM((2 * EACH * BLOCKS, LANES), F32),
-            pltpu.VMEM((BUFFERS, 2 * PHASES, BLOCKS + PAD, LANES), F32),
-            pltpu.VMEM((BUFFERS, 2 * PHASES, BLOCKS + PAD, LANES), F32),
-            pltpu.VMEM((BUFFERS, 3 * (PHASES - 1), BLOCKS + PAD, LANES), F32),
-            pltpu.VMEM((BUFFERS, 3, BLOCKS + PAD, LANES), F32),
+            pltpu.VMEM((EACH, 2 * PHASES * BLOCKS, BLOCKS * STEP), BF16),
+            pltpu.VMEM((EACH, 2 * PHASES * BLOCKS, 2 * LANES), F32),
         ],
     )(table, columns)
     back = lax.all_to_all(results, OWNERS, split_axis=0, concat_axis=0, tiled=True)

time: 39.9 us -> 39.2 us (0.982)
  Pallas kernels: 3.93 us -> 3.23 us
    pallas_call x1, Pallas kernels: 2.2 us -> 1.5 us  [shards(): pl.pallas_call(middle_kernel, name='middle', compiler_params=grant(12), o...]
where the time goes in v6:
time: 39.2 us; the launch traced here: 39 us
  blocking collectives  35.1 us (90%)
  Pallas kernels  3.23 us (8%)
  between operations  0.65 us (2%)
    all_to_all x1, blocking collectives, shards(): lax.all_to_all(parts.reshape(BLOCKS, IN_ROWS, LANES), SEQ, split_axis=0,...  26.9 us
    all_to_all x1, blocking collectives, shards(): lax.all_to_all(results, OWNERS, split_axis=0, concat_axis=0, tiled=True)  8.22 us
    pallas_call x1, Pallas kernels, shards(): pl.pallas_call(middle_kernel, name='middle', compiler_params=grant(12), o...  1.5 us
    pallas_call x1, Pallas kernels, shards(): pl.pallas_call(pack_kernel, name='pack', compiler_params=grant(4), out_sh...  1 us

profile of v6, /device:TPU:1, one launch (start us, length us, event | category | flops | bytes accessed | tf_op | source)
XLA Modules:
  0.0 39.0 jit_solution(15823701296053542239)
XLA Ops:
  0.6 1.0 %pack.1 = (bf16[4,2,2,40,128]{4,3,2,1,0:T(8,128)(2,1)S(1)}, f32[10,8,128]{2,1,0:T(8,128)S(1)}) custom-call(bf16[3,4,2,8,128]{4,3,2,1,0:T(8,128)(2,1)} %bitcast.12, bf16[4,2,8,128]{3,2,1,0:T(8,128)(2,1)} %bitcast.13, bf16[4,2,8,128]{3,2,1,0:T(8,128)(2,1)} %bitcast.14, f32[3,3,64]{2,1,0:T(4,128)} %bitcast.15, f32[1,64]{1,0:T(1,128)} %bitcast.16), custom_call_target="tpu_custom_call" | custom-call | tf_op jit(solution)/shard_map/pack/pallas_call | solution.py:318
  1.6 26.9 %all_to_all.10.received = bf16[16,40,128]{2,1,0:T(8,128)(2,1)S(1)} all-to-all(bf16[16,40,128]{2,1,0:T(8,128)(2,1)S(1)} %bitcast.11), channel_id=1, replica_groups=mesh['x'=4,'y'=2,'c'=2,'chan'=64] {'x','y','c'}, dimensions={0} | all-to-all | bytes 327680 | tf_op jit(solution)/shard_map/all_to_all | solution.py:340
  28.5 1.5 %middle.1 = bf16[8,56,128]{2,1,0:T(8,128)(2,1)S(1)} custom-call(f32[10,8,128]{2,1,0:T(8,128)S(1)} %get-tuple-element.12.table, bf16[16,40,128]{2,1,0:T(8,128)(2,1)S(1)} %all_to_all.10.received), custom_call_target="tpu_custom_call" | custom-call | tf_op jit(solution)/shard_map/middle/pallas_call | solution.py:343
  30.0 8.2 %all_to_all.11.received = bf16[8,56,128]{2,1,0:T(8,128)(2,1)S(1)} all-to-all(bf16[8,56,128]{2,1,0:T(8,128)(2,1)S(1)} %middle.1), channel_id=1, replica_groups=mesh['x'=4,'y'=2,'c'=2,'chan'=64] {'x','c'}, dimensions={0} | all-to-all | bytes 229376 | tf_op jit(solution)/shard_map/all_to_all | solution.py:361
  38.2 0.7 %unpack.1 = (bf16[8,8,128]{2,1,0:T(8,128)(2,1)}, bf16[3,8,8,128]{3,2,1,0:T(8,128)(2,1)}, bf16[8,8,128]{2,1,0:T(8,128)(2,1)}, f32[3,3,64]{2,1,0:T(4,128)}, f32[1,64]{1,0:T(1,128)}) custom-call(bf16[8,56,128]{2,1,0:T(8,128)(2,1)S(1)} %all_to_all.11.received), custom_call_target="tpu_custom_call" | custom-call | tf_op jit(solution)/shard_map/unpack/pallas_call | solution.py:363

commit v7 on v6

--- a/solution.py
+++ b/solution.py
@@ -8,7 +8,8 @@
 
 SEQ = ("x", "y", "c")
 SIDES = (4, 2, 2)
-OWNERS = ("x", "c")
+ENTRY = ("c", "y", "x")
+OWNERS = ("c", "x")
 BLOCKS = 16
 GROUPS = 8
 EACH = 8
@@ -44,7 +45,7 @@
         copy.start()
     for copy in small:
         copy.wait()
-    first = (lax.axis_index("x") * SIDES[2] + lax.axis_index("c")) * EACH
+    first = (lax.axis_index("c") * SIDES[0] + lax.axis_index("x")) * EACH
     channels = gains.shape[1]
     shape = (EACH, channels)
     chosen = iota(shape, 1) == iota(shape, 0) + first
@@ -132,9 +133,12 @@
     pad = jnp.zeros((IN_ROWS, LANES), F32)
     wide[0:IN_ROWS, :] = pad
     wide[(BLOCKS + 1) * IN_ROWS : (BLOCKS + 2) * IN_ROWS, :] = pad
-    wide[IN_ROWS : (BLOCKS + 1) * IN_ROWS, :] = (
-        received[...].astype(F32).reshape(BLOCKS * IN_ROWS, LANES)
-    )
+    for c in range(SIDES[2]):
+        for y in range(SIDES[1]):
+            for x in range(SIDES[0]):
+                source = (c * SIDES[1] + y) * SIDES[0] + x
+                at = ((x * SIDES[1] + y) * SIDES[2] + c + 1) * IN_ROWS
+                wide[at : at + IN_ROWS, :] = received[source].astype(F32)
     square = (LANES, LANES)
     mirror = jnp.where(iota(square, 0) + iota(square, 1) == LANES - 1, 1.0, 0.0).astype(BF16)
 
@@ -260,19 +264,18 @@
     totals = jnp.broadcast_to(totals, stacked.shape).reshape(shape)
     channels = GROUPS * EACH
     lane = iota(shape, 2)
-    first = (lax.axis_index("x") * SIDES[2] + lax.axis_index("c")) * EACH
+    first = (lax.axis_index("c") * SIDES[0] + lax.axis_index("x")) * EACH
     both = jnp.where(lane < channels, upper, totals - upper)
     mine = lane % channels == iota(shape, 1) + first
     lines = jnp.sum(jnp.where(mine, both, 0.0), axis=1)
     rest = jnp.zeros((OUT_ROWS - IN_ROWS - SUMS, LANES), F32)
     lines = jnp.concatenate([lines, rest], axis=0).astype(BF16)
     side = lax.axis_index("y")
-    wanted = SIDES[2] * IN_ROWS
-    for x in range(SIDES[0]):
-        at = pl.multiple_of((SIDES[1] * x + side) * wanted, 8)
-        block = packed[pl.ds(at, wanted), :].astype(BF16)
-        target = slice(SIDES[2] * x, SIDES[2] * (x + 1))
-        out[target, 0:IN_ROWS, :] = block.reshape(SIDES[2], IN_ROWS, LANES)
+    for c in range(SIDES[2]):
+        for x in range(SIDES[0]):
+            block = (x * SIDES[1] + side) * SIDES[2] + c
+            at = pl.multiple_of(block * IN_ROWS, 8)
+            out[c * SIDES[0] + x, 0:IN_ROWS, :] = packed[pl.ds(at, IN_ROWS), :].astype(BF16)
     for n in range(GROUPS):
         out[n, IN_ROWS:OUT_ROWS, :] = lines
 
@@ -314,13 +317,13 @@
     channels = features.shape[1]
     whole = pl.BlockSpec(memory_space=pltpu.VMEM)
     far = pl.BlockSpec(memory_space=pltpu.HBM)
-    cut = (SIDES[0], SIDES[2], EACH, LANES)
+    cut = (SIDES[2], SIDES[0], EACH, LANES)
     parts, table = pl.pallas_call(
         pack_kernel,
         name="pack",
         compiler_params=grant(4),
         out_shape=(
-            jax.ShapeDtypeStruct((*SIDES, IN_ROWS, LANES), BF16),
+            jax.ShapeDtypeStruct((*SIDES[::-1], IN_ROWS, LANES), BF16),
             jax.ShapeDtypeStruct((SUMS, EACH, LANES), F32),
         ),
         in_specs=[far] * 5,
@@ -338,7 +341,7 @@
         stay(skip_gain.reshape(1, channels)),
     )
     columns = lax.all_to_all(
-        parts.reshape(BLOCKS, IN_ROWS, LANES), SEQ, split_axis=0, concat_axis=0, tiled=True
+        parts.reshape(BLOCKS, IN_ROWS, LANES), ENTRY, split_axis=0, concat_axis=0, tiled=True
     )
     results = pl.pallas_call(
         middle_kernel,

time: 39.2 us -> 39.2 us (level)
  no operation moved by 1% of the time
where the time goes in v7:
time: 39.2 us; the launch traced here: 39 us
  blocking collectives  35.1 us (90%)
  Pallas kernels  3.23 us (8%)
  between operations  0.64 us (2%)
    all_to_all x1, blocking collectives, shards(): lax.all_to_all(parts.reshape(BLOCKS, IN_ROWS, LANES), ENTRY, split_axis=0...  27.2 us
    all_to_all x1, blocking collectives, shards(): lax.all_to_all(results, OWNERS, split_axis=0, concat_axis=0, tiled=True)  7.9 us
    pallas_call x1, Pallas kernels, shards(): pl.pallas_call(middle_kernel, name='middle', compiler_params=grant(12), o...  1.5 us
    pallas_call x1, Pallas kernels, shards(): pl.pallas_call(pack_kernel, name='pack', compiler_params=grant(4), out_sh...  1 us

profile of v7, /device:TPU:1, one launch (start us, length us, event | category | flops | bytes accessed | tf_op | source)
XLA Modules:
  0.0 39.0 jit_solution(17423199588816436933)
XLA Ops:
  0.6 1.0 %pack.1 = (bf16[2,2,4,40,128]{4,3,2,1,0:T(8,128)(2,1)S(1)}, f32[10,8,128]{2,1,0:T(8,128)S(1)}) custom-call(bf16[3,2,4,8,128]{4,3,2,1,0:T(8,128)(2,1)} %bitcast.12, bf16[2,4,8,128]{3,2,1,0:T(8,128)(2,1)} %bitcast.13, bf16[2,4,8,128]{3,2,1,0:T(8,128)(2,1)} %bitcast.14, f32[3,3,64]{2,1,0:T(4,128)} %bitcast.15, f32[1,64]{1,0:T(1,128)} %bitcast.16), custom_call_target="tpu_custom_call" | custom-call | tf_op jit(solution)/shard_map/pack/pallas_call | solution.py:321
  1.6 27.2 %all_to_all.10.received = bf16[16,40,128]{2,1,0:T(8,128)(2,1)S(1)} all-to-all(bf16[16,40,128]{2,1,0:T(8,128)(2,1)S(1)} %bitcast.11), channel_id=1, replica_groups=mesh['x'=4,'y'=2,'c'=2,'chan'=64] {'c','y','x'}, dimensions={0} | all-to-all | bytes 327680 | tf_op jit(solution)/shard_map/all_to_all | solution.py:343
  28.8 1.5 %middle.1 = bf16[8,56,128]{2,1,0:T(8,128)(2,1)S(1)} custom-call(f32[10,8,128]{2,1,0:T(8,128)S(1)} %get-tuple-element.12.table, bf16[16,40,128]{2,1,0:T(8,128)(2,1)S(1)} %all_to_all.10.received), custom_call_target="tpu_custom_call" | custom-call | tf_op jit(solution)/shard_map/middle/pallas_call | solution.py:346
  30.3 7.9 %all_to_all.11.received = bf16[8,56,128]{2,1,0:T(8,128)(2,1)S(1)} all-to-all(bf16[8,56,128]{2,1,0:T(8,128)(2,1)S(1)} %middle.1), channel_id=1, replica_groups=mesh['x'=4,'y'=2,'c'=2,'chan'=64] {'c','x'}, dimensions={0} | all-to-all | bytes 229376 | tf_op jit(solution)/shard_map/all_to_all | solution.py:364
  38.2 0.7 %unpack.1 = (bf16[8,8,128]{2,1,0:T(8,128)(2,1)}, bf16[3,8,8,128]{3,2,1,0:T(8,128)(2,1)}, bf16[8,8,128]{2,1,0:T(8,128)(2,1)}, f32[3,3,64]{2,1,0:T(4,128)}, f32[1,64]{1,0:T(1,128)}) custom-call(bf16[8,56,128]{2,1,0:T(8,128)(2,1)S(1)} %all_to_all.11.received), custom_call_target="tpu_custom_call" | custom-call | tf_op jit(solution)/shard_map/unpack/pallas_call | solution.py:366

commit v8 on v7

--- a/solution.py
+++ b/solution.py
@@ -38,9 +38,8 @@
     sources = [features.at[i] for i in range(3)] + [cotangent, long_filter]
     large = []
     for i, source in enumerate(sources):
-        for y in range(SIDES[1]):
-            target = out.at[:, y, :, pl.ds(i * EACH, EACH), :]
-            large.append(pltpu.make_async_copy(source, target, sems.at[2 + 2 * i + y]))
+        target = out.at[:, 0, :, pl.ds(i * EACH, EACH), :]
+        large.append(pltpu.make_async_copy(source, target, sems.at[2 + i]))
     for copy in small + large:
         copy.start()
     for copy in small:
@@ -56,6 +55,7 @@
         table[j] = jnp.broadcast_to(column, (EACH, LANES))
     for copy in large:
         copy.wait()
+    out[:, 1] = out[:, 0]
 
 
 def after(values, before, count):
@@ -128,7 +128,7 @@
 
 
 def middle_kernel(
-    table, received, out, wide, packed, right, kept, mirrored, turned_back, left, product
+    table, received, out, wide, packed, right, kept, mirrored, turned_back, left, product, sums
 ):
     pad = jnp.zeros((IN_ROWS, LANES), F32)
     wide[0:IN_ROWS, :] = pad
@@ -157,7 +157,10 @@
 
     PRIMED, MIXED, GATED, HISTORY, LONG = 0, 3, 4, 5, 11
     half = EACH * BLOCKS
-    sums = [[] for _ in range(SUMS)]
+
+    def add(j, c, values):
+        at = (j * EACH + c) * 8
+        sums[at : at + 8, :] = values[0:8] + values[8:16]
 
     def prime(c):
         primed = []
@@ -234,9 +237,8 @@
             put(1 + i, c, running)
             for o in range(TAPS):
                 past = kept[HISTORY + 2 * i + o - 1, rows(c), :] if o else stream(i, c)
-                sums[i * TAPS + o].append(jnp.sum(primed_grad[i] * past, axis=0, keepdims=True))
-        both = kept[GATED, rows(c), :] * kept[MIXED, rows(c), :]
-        sums[3 * TAPS].append(jnp.sum(both, axis=0, keepdims=True))
+                add(i * TAPS + o, c, primed_grad[i] * past)
+        add(3 * TAPS, c, kept[GATED, rows(c), :] * kept[MIXED, rows(c), :])
 
     for c in range(EACH):
         prime(c)
@@ -256,7 +258,13 @@
         turn_back(c)
     for c in range(EACH):
         finish(c)
-    stacked = jnp.concatenate([line for lines in sums for line in lines], axis=0)
+    lines = []
+    for j in range(SUMS):
+        line = sums[pl.ds(j * EACH * 8, EACH, stride=8), :]
+        for n in range(1, 8):
+            line = line + sums[pl.ds(j * EACH * 8 + n, EACH, stride=8), :]
+        lines.append(line)
+    stacked = jnp.concatenate(lines, axis=0)
     totals = jnp.sum(stacked, axis=1, keepdims=True)
     upper = totals.astype(BF16).astype(F32)
     shape = (SUMS, EACH, LANES)
@@ -331,7 +339,7 @@
         scratch_shapes=[
             pltpu.VMEM((3, TAPS, channels), F32),
             pltpu.VMEM((1, channels), F32),
-            pltpu.SemaphoreType.DMA((2 + 2 * STREAMS,)),
+            pltpu.SemaphoreType.DMA((2 + STREAMS,)),
         ],
     )(
         stay(features.reshape(3, *cut)),
@@ -359,6 +367,7 @@
             pltpu.VMEM((2 * EACH * BLOCKS, LANES), F32),
             pltpu.VMEM((EACH, 2 * PHASES * BLOCKS, BLOCKS * STEP), BF16),
             pltpu.VMEM((EACH, 2 * PHASES * BLOCKS, 2 * LANES), F32),
+            pltpu.VMEM((SUMS * EACH * 8, LANES), F32),
         ],
     )(table, columns)
     back = lax.all_to_all(results, OWNERS, split_axis=0, concat_axis=0, tiled=True)

time: 39.2 us -> 39.1 us (level)
  no operation moved by 1% of the time
where the time goes in v8:
time: 39.1 us; the launch traced here: 38.8 us
  blocking collectives  35.1 us (90%)
  Pallas kernels  3.11 us (8%)
  between operations  0.65 us (2%)
    all_to_all x1, blocking collectives, shards(): lax.all_to_all(parts.reshape(BLOCKS, IN_ROWS, LANES), ENTRY, split_axis=0...  27.2 us
    all_to_all x1, blocking collectives, shards(): lax.all_to_all(results, OWNERS, split_axis=0, concat_axis=0, tiled=True)  7.9 us
    pallas_call x1, Pallas kernels, shards(): pl.pallas_call(middle_kernel, name='middle', compiler_params=grant(12), o...  1.48 us
    pallas_call x1, Pallas kernels, shards(): pl.pallas_call(pack_kernel, name='pack', compiler_params=grant(4), out_sh...  0.89 us

profile of v8, /device:TPU:1, one launch (start us, length us, event | category | flops | bytes accessed | tf_op | source)
XLA Modules:
  0.0 38.8 jit_solution(7106639245378758142)
XLA Ops:
  0.6 0.9 %pack.1 = (bf16[2,2,4,40,128]{4,3,2,1,0:T(8,128)(2,1)S(1)}, f32[10,8,128]{2,1,0:T(8,128)S(1)}) custom-call(bf16[3,2,4,8,128]{4,3,2,1,0:T(8,128)(2,1)} %bitcast.12, bf16[2,4,8,128]{3,2,1,0:T(8,128)(2,1)} %bitcast.13, bf16[2,4,8,128]{3,2,1,0:T(8,128)(2,1)} %bitcast.14, f32[3,3,64]{2,1,0:T(4,128)} %bitcast.15, f32[1,64]{1,0:T(1,128)} %bitcast.16), custom_call_target="tpu_custom_call" | custom-call | tf_op jit(solution)/shard_map/pack/pallas_call | solution.py:329
  1.5 27.2 %all_to_all.10.received = bf16[16,40,128]{2,1,0:T(8,128)(2,1)S(1)} all-to-all(bf16[16,40,128]{2,1,0:T(8,128)(2,1)S(1)} %bitcast.11), channel_id=1, replica_groups=mesh['x'=4,'y'=2,'c'=2,'chan'=64] {'c','y','x'}, dimensions={0} | all-to-all | bytes 327680 | tf_op jit(solution)/shard_map/all_to_all | solution.py:351
  28.7 1.5 %middle.1 = bf16[8,56,128]{2,1,0:T(8,128)(2,1)S(1)} custom-call(f32[10,8,128]{2,1,0:T(8,128)S(1)} %get-tuple-element.12.table, bf16[16,40,128]{2,1,0:T(8,128)(2,1)S(1)} %all_to_all.10.received), custom_call_target="tpu_custom_call" | custom-call | tf_op jit(solution)/shard_map/middle/pallas_call | solution.py:354
  30.2 7.9 %all_to_all.11.received = bf16[8,56,128]{2,1,0:T(8,128)(2,1)S(1)} all-to-all(bf16[8,56,128]{2,1,0:T(8,128)(2,1)S(1)} %middle.1), channel_id=1, replica_groups=mesh['x'=4,'y'=2,'c'=2,'chan'=64] {'c','x'}, dimensions={0} | all-to-all | bytes 229376 | tf_op jit(solution)/shard_map/all_to_all | solution.py:373
  38.1 0.7 %unpack.1 = (bf16[8,8,128]{2,1,0:T(8,128)(2,1)}, bf16[3,8,8,128]{3,2,1,0:T(8,128)(2,1)}, bf16[8,8,128]{2,1,0:T(8,128)(2,1)}, f32[3,3,64]{2,1,0:T(4,128)}, f32[1,64]{1,0:T(1,128)}) custom-call(bf16[8,56,128]{2,1,0:T(8,128)(2,1)S(1)} %all_to_all.11.received), custom_call_target="tpu_custom_call" | custom-call | tf_op jit(solution)/shard_map/unpack/pallas_call | solution.py:375

commit v9 on v8

--- a/solution.py
+++ b/solution.py
@@ -53,9 +53,10 @@
         line = jnp.broadcast_to(line, shape)
         column = jnp.sum(jnp.where(chosen, line, 0.0), axis=1, keepdims=True)
         table[j] = jnp.broadcast_to(column, (EACH, LANES))
-    for copy in large:
+    for i, copy in enumerate(large):
         copy.wait()
-    out[:, 1] = out[:, 0]
+        cut = slice(i * EACH, (i + 1) * EACH)
+        out[:, 1, :, cut, :] = out[:, 0, :, cut, :]
 
 
 def after(values, before, count):

time: 39.1 us -> 39.1 us (level)
  no operation moved by 1% of the time
where the time goes in v9:
time: 39.1 us; the launch traced here: 38.8 us
  blocking collectives  35.1 us (90%)
  Pallas kernels  3.1 us (8%)
  between operations  0.65 us (2%)
    all_to_all x1, blocking collectives, shards(): lax.all_to_all(parts.reshape(BLOCKS, IN_ROWS, LANES), ENTRY, split_axis=0...  27.2 us
    all_to_all x1, blocking collectives, shards(): lax.all_to_all(results, OWNERS, split_axis=0, concat_axis=0, tiled=True)  7.9 us
    pallas_call x1, Pallas kernels, shards(): pl.pallas_call(middle_kernel, name='middle', compiler_params=grant(12), o...  1.48 us
    pallas_call x1, Pallas kernels, shards(): pl.pallas_call(pack_kernel, name='pack', compiler_params=grant(4), out_sh...  0.88 us

profile of v9, /device:TPU:1, one launch (start us, length us, event | category | flops | bytes accessed | tf_op | source)
XLA Modules:
  0.0 38.8 jit_solution(6026034336053691737)
XLA Ops:
  0.6 0.9 %pack.1 = (bf16[2,2,4,40,128]{4,3,2,1,0:T(8,128)(2,1)S(1)}, f32[10,8,128]{2,1,0:T(8,128)S(1)}) custom-call(bf16[3,2,4,8,128]{4,3,2,1,0:T(8,128)(2,1)} %bitcast.12, bf16[2,4,8,128]{3,2,1,0:T(8,128)(2,1)} %bitcast.13, bf16[2,4,8,128]{3,2,1,0:T(8,128)(2,1)} %bitcast.14, f32[3,3,64]{2,1,0:T(4,128)} %bitcast.15, f32[1,64]{1,0:T(1,128)} %bitcast.16), custom_call_target="tpu_custom_call" | custom-call | tf_op jit(solution)/shard_map/pack/pallas_call | solution.py:330
  1.5 27.2 %all_to_all.10.received = bf16[16,40,128]{2,1,0:T(8,128)(2,1)S(1)} all-to-all(bf16[16,40,128]{2,1,0:T(8,128)(2,1)S(1)} %bitcast.11), channel_id=1, replica_groups=mesh['x'=4,'y'=2,'c'=2,'chan'=64] {'c','y','x'}, dimensions={0} | all-to-all | bytes 327680 | tf_op jit(solution)/shard_map/all_to_all | solution.py:352
  28.7 1.5 %middle.1 = bf16[8,56,128]{2,1,0:T(8,128)(2,1)S(1)} custom-call(f32[10,8,128]{2,1,0:T(8,128)S(1)} %get-tuple-element.12.table, bf16[16,40,128]{2,1,0:T(8,128)(2,1)S(1)} %all_to_all.10.received), custom_call_target="tpu_custom_call" | custom-call | tf_op jit(solution)/shard_map/middle/pallas_call | solution.py:355
  30.2 7.9 %all_to_all.11.received = bf16[8,56,128]{2,1,0:T(8,128)(2,1)S(1)} all-to-all(bf16[8,56,128]{2,1,0:T(8,128)(2,1)S(1)} %middle.1), channel_id=1, replica_groups=mesh['x'=4,'y'=2,'c'=2,'chan'=64] {'c','x'}, dimensions={0} | all-to-all | bytes 229376 | tf_op jit(solution)/shard_map/all_to_all | solution.py:374
  38.1 0.7 %unpack.1 = (bf16[8,8,128]{2,1,0:T(8,128)(2,1)}, bf16[3,8,8,128]{3,2,1,0:T(8,128)(2,1)}, bf16[8,8,128]{2,1,0:T(8,128)(2,1)}, f32[3,3,64]{2,1,0:T(4,128)}, f32[1,64]{1,0:T(1,128)}) custom-call(bf16[8,56,128]{2,1,0:T(8,128)(2,1)S(1)} %all_to_all.11.received), custom_call_target="tpu_custom_call" | custom-call | tf_op jit(solution)/shard_map/unpack/pallas_call | solution.py:376

commit v10 on v8

--- a/solution.py
+++ b/solution.py
@@ -240,10 +240,11 @@
                 add(i * TAPS + o, c, primed_grad[i] * past)
         add(3 * TAPS, c, kept[GATED, rows(c), :] * kept[MIXED, rows(c), :])
 
-    for c in range(EACH):
-        prime(c)
-    for c in range(EACH):
-        turn(c)
+    for c in range(EACH + 4):
+        if 0 <= c < EACH + 0:
+            prime(c - 0)
+        if 4 <= c < EACH + 4:
+            turn(c - 4)
     for c in range(EACH):
         filter_band(c)
         mixed_rows(c)
@@ -254,10 +255,11 @@
         multiply(c)
     for c in range(EACH):
         gather(c)
-    for c in range(EACH):
-        turn_back(c)
-    for c in range(EACH):
-        finish(c)
+    for c in range(EACH + 4):
+        if 0 <= c < EACH + 0:
+            turn_back(c - 0)
+        if 4 <= c < EACH + 4:
+            finish(c - 4)
     lines = []
     for j in range(SUMS):
         line = sums[pl.ds(j * EACH * 8, EACH, stride=8), :]

time: 39.1 us -> 39.1 us (level)
  no operation moved by 1% of the time
where the time goes in v10:
time: 39.1 us; the launch traced here: 38.8 us
  blocking collectives  35.1 us (90%)
  Pallas kernels  3.11 us (8%)
  between operations  0.65 us (2%)
    all_to_all x1, blocking collectives, shards(): lax.all_to_all(parts.reshape(BLOCKS, IN_ROWS, LANES), ENTRY, split_axis=0...  27.2 us
    all_to_all x1, blocking collectives, shards(): lax.all_to_all(results, OWNERS, split_axis=0, concat_axis=0, tiled=True)  7.9 us
    pallas_call x1, Pallas kernels, shards(): pl.pallas_call(middle_kernel, name='middle', compiler_params=grant(12), o...  1.48 us
    pallas_call x1, Pallas kernels, shards(): pl.pallas_call(pack_kernel, name='pack', compiler_params=grant(4), out_sh...  0.89 us

profile of v10, /device:TPU:1, one launch (start us, length us, event | category | flops | bytes accessed | tf_op | source)
XLA Modules:
  0.0 38.8 jit_solution(7106639245378758142)
XLA Ops:
  0.6 0.9 %pack.1 = (bf16[2,2,4,40,128]{4,3,2,1,0:T(8,128)(2,1)S(1)}, f32[10,8,128]{2,1,0:T(8,128)S(1)}) custom-call(bf16[3,2,4,8,128]{4,3,2,1,0:T(8,128)(2,1)} %bitcast.12, bf16[2,4,8,128]{3,2,1,0:T(8,128)(2,1)} %bitcast.13, bf16[2,4,8,128]{3,2,1,0:T(8,128)(2,1)} %bitcast.14, f32[3,3,64]{2,1,0:T(4,128)} %bitcast.15, f32[1,64]{1,0:T(1,128)} %bitcast.16), custom_call_target="tpu_custom_call" | custom-call | tf_op jit(solution)/shard_map/pack/pallas_call | solution.py:331
  1.5 27.2 %all_to_all.10.received = bf16[16,40,128]{2,1,0:T(8,128)(2,1)S(1)} all-to-all(bf16[16,40,128]{2,1,0:T(8,128)(2,1)S(1)} %bitcast.11), channel_id=1, replica_groups=mesh['x'=4,'y'=2,'c'=2,'chan'=64] {'c','y','x'}, dimensions={0} | all-to-all | bytes 327680 | tf_op jit(solution)/shard_map/all_to_all | solution.py:353
  28.7 1.5 %middle.1 = bf16[8,56,128]{2,1,0:T(8,128)(2,1)S(1)} custom-call(f32[10,8,128]{2,1,0:T(8,128)S(1)} %get-tuple-element.12.table, bf16[16,40,128]{2,1,0:T(8,128)(2,1)S(1)} %all_to_all.10.received), custom_call_target="tpu_custom_call" | custom-call | tf_op jit(solution)/shard_map/middle/pallas_call | solution.py:356
  30.2 7.9 %all_to_all.11.received = bf16[8,56,128]{2,1,0:T(8,128)(2,1)S(1)} all-to-all(bf16[8,56,128]{2,1,0:T(8,128)(2,1)S(1)} %middle.1), channel_id=1, replica_groups=mesh['x'=4,'y'=2,'c'=2,'chan'=64] {'c','x'}, dimensions={0} | all-to-all | bytes 229376 | tf_op jit(solution)/shard_map/all_to_all | solution.py:375
  38.1 0.7 %unpack.1 = (bf16[8,8,128]{2,1,0:T(8,128)(2,1)}, bf16[3,8,8,128]{3,2,1,0:T(8,128)(2,1)}, bf16[8,8,128]{2,1,0:T(8,128)(2,1)}, f32[3,3,64]{2,1,0:T(4,128)}, f32[1,64]{1,0:T(1,128)}) custom-call(bf16[8,56,128]{2,1,0:T(8,128)(2,1)S(1)} %all_to_all.11.received), custom_call_target="tpu_custom_call" | custom-call | tf_op jit(solution)/shard_map/unpack/pallas_call | solution.py:377
